TPU v7x, 32 devices: a whole 2x2x4 slice. The times are simulated.
32 devices in a mesh: seq: 16 (over z, x, core), fsdp: 2 (over y).
Axes of the slice: x: 2, y: 2, z: 4, core: 2. Of those that a mesh axis runs over, the one named last changes fastest.
Arguments:
- hidden_next: bfloat16 [4096, 8192], P('seq'), may hold values from -6 to 6
- values_next: bfloat16 [4096, 8192], P('seq', 'fsdp'), may hold values from -6 to 6
- seg_next: int32 [4], replicated, may hold values from 1 to 2048, 4096 in all
- proj_bc: bfloat16 [8192, 1024], P(('seq', 'fsdp')), may hold values from -0.046875 to 0.046875
- proj_dt: bfloat16 [8192, 128], P(('seq', 'fsdp')), may hold values from -0.0625 to 0.0625
- dt_bias: float32 [128], replicated, may hold values from -4 to -2.5
- decay_rate: float32 [128], replicated, may hold values from 0 to 1, as said below
- skip_gain: float32 [128], replicated, may hold values from 0.5 to 1.5
- bc_prev: bfloat16 [4096, 1024], P('seq'), may hold values from -4 to 4
- dt_prev: float32 [4096, 128], P('seq', 'fsdp'), may hold values from 0.01 to 0.3
- seg_prev: int32 [4], replicated, may hold values from 1 to 2048, 4096 in all
- grad_prev: bfloat16 [4096, 8192], P('seq', 'fsdp'), may hold values from -6 to 6
Outputs:
- out_next: bfloat16 [4096, 8192], P('seq', 'fsdp')
- grad_values: bfloat16 [4096, 8192], P('seq', 'fsdp')
Inputs may be any that keep to these rules, and one draw needn't show every extreme that they name: `seg_next`: lengths of the rollout's 4 segments in order, summing to 4096. `seg_prev`: lengths of the rollout's 4 segments in order, summing to 4096. `decay_rate`: positive.
All inputs are finite; a program needn't handle non-finite values.
Results may differ from a plain program's by a relative error of at most 0.0064.
Values may be sent and summed in bfloat16 or wider, within the bound.
A program may use at most 192 MiB of HBM per device.

v0:
```python
import jax
import jax.numpy as jnp
from jax import lax
from jax.sharding import PartitionSpec as P

GW = 4
SPAN = 128


def entering_2(part, axis, combine, identity, reverse):
    count = lax.axis_size(axis)
    place = lax.axis_index(axis)
    ahead = count - 1 - place if reverse else place
    gathered = jax.tree.map(lambda a: lax.all_gather(a, axis), part)
    state = jax.tree.map(lambda a, e: jnp.zeros_like(a) + jnp.asarray(e, a.dtype), part, identity)

    def one(lap, state):
        source = count - 1 - lap if reverse else lap
        return combine(
            state, jax.tree.map(lambda a: lax.dynamic_index_in_dim(a, source, 0, False), gathered)
        )

    return lax.fori_loop(0, ahead, one, state)


def joined(earlier, later):
    return (earlier[0] * later[0], later[0][:, None] * earlier[1] + later[1])


def segment_marks(lengths, offset, length):
    bounds = jnp.cumsum(lengths)[:-1]
    places = offset + jnp.arange(length + 1, dtype=jnp.int32) - 1
    return jnp.sum((bounds[None, :] <= places[:, None]).astype(jnp.int32), axis=1)


def pick_groups(bc_rows, first_group, groups_dev, nblocks):
    tokens_dev, width_all = bc_rows.shape
    state_dim = width_all // (2 * GW)
    halves = bc_rows.reshape(tokens_dev, 2, GW, state_dim)
    picked = lax.dynamic_slice_in_dim(halves, first_group, groups_dev, 2)
    b_vectors = picked[:, 0].reshape(nblocks, tokens_dev // nblocks, groups_dev, state_dim)
    c_vectors = picked[:, 1].reshape(nblocks, tokens_dev // nblocks, groups_dev, state_dim)
    return (b_vectors, c_vectors)


def block_parts(b_vectors, c_vectors, dt_blocks, marks_all, decay_local):
    nblocks, span_len, groups, state_dim = b_vectors.shape
    heads_dev = dt_blocks.shape[2]
    segment = marks_all[1:].reshape(nblocks, span_len)
    before = marks_all[:-1].reshape(nblocks, span_len)[:, 0]
    cumulative = jnp.cumsum(-dt_blocks * decay_local, axis=1)
    final_cum = cumulative[:, -1]
    places = jnp.arange(span_len)
    linked = (segment[:, :, None] == segment[:, None, :]) & (places[:, None] >= places[None, :])
    scores = jnp.einsum("ktgn,ksgn->kgts", c_vectors, b_vectors, preferred_element_type=jnp.float32)
    by_head = jnp.swapaxes(cumulative, 1, 2)
    spread = by_head[:, :, :, None] - by_head[:, :, None, :]
    decays = jnp.exp(jnp.where(linked[:, None], spread, -jnp.inf))
    weighted = (decays * jnp.swapaxes(dt_blocks, 1, 2)[:, :, None, :]).reshape(
        nblocks, groups, heads_dev // groups, span_len, span_len
    )
    mixing = (
        (weighted * scores[:, :, None])
        .reshape(nblocks, heads_dev, span_len, span_len)
        .astype(jnp.bfloat16)
    )
    keep_final = (segment == segment[:, -1:]).astype(jnp.float32)
    linked_in = (segment == before[:, None]).astype(jnp.float32)
    send_factor = keep_final[:, :, None] * jnp.exp(final_cum[:, None, :] - cumulative) * dt_blocks
    read_factor = linked_in[:, :, None] * jnp.exp(cumulative)
    carry_decay = (segment[:, -1] == before).astype(jnp.float32)[:, None] * jnp.exp(final_cum)
    return (mixing, send_factor, read_factor, carry_decay)


def outer_sum(values, vectors):
    nblocks, span_len, heads_dev, head_dim = values.shape
    groups = vectors.shape[2]
    grouped = values.reshape(nblocks, span_len, groups, heads_dev // groups, head_dim)
    result = jnp.einsum("ksgqp,ksgn->kgqpn", grouped, vectors, preferred_element_type=jnp.float32)
    return result.reshape(nblocks, heads_dev, head_dim * vectors.shape[3])


def read_state(state_now, vectors, factor):
    nblocks, heads_dev, head_dim, state_dim = state_now.shape
    groups = vectors.shape[2]
    grouped = state_now.reshape(nblocks, groups, heads_dev // groups, head_dim, state_dim)
    result = jnp.einsum(
        "kgqpn,ktgn->ktgqp", grouped, vectors.astype(jnp.float32), precision=lax.Precision.HIGHEST
    )
    return result.reshape(nblocks, vectors.shape[1], heads_dev, head_dim) * factor[:, :, :, None]


def body(
    hidden_next,
    values_next,
    seg_next,
    proj_bc,
    proj_dt,
    dt_bias,
    decay_rate,
    skip_gain,
    bc_prev,
    dt_prev,
    seg_prev,
    grad_prev,
):
    tokens_dev = hidden_next.shape[0]
    bc_width = proj_bc.shape[1]
    heads_all = proj_dt.shape[1]
    fsdp_count = lax.axis_size("fsdp")
    fsdp_place = lax.axis_index("fsdp")
    heads_dev = heads_all // fsdp_count
    head_dim = values_next.shape[1] // heads_dev
    state_dim = bc_width // (2 * GW)
    flat_size = head_dim * state_dim
    per_group = heads_all // GW
    groups_dev = max(1, heads_dev // per_group)
    first_head = fsdp_place * heads_dev
    first_group = first_head // per_group
    rows_dev = proj_bc.shape[0]
    seq_count = lax.axis_size("seq")
    arranged = hidden_next.reshape(tokens_dev, seq_count, fsdp_count, rows_dev)
    owned = lax.dynamic_slice_in_dim(arranged, fsdp_place, 1, 2).reshape(
        tokens_dev, seq_count * rows_dev
    )
    bc_sum, dt_sum = lax.psum(
        (
            jnp.dot(
                owned,
                lax.all_gather(proj_bc, "seq", axis=0, tiled=True),
                preferred_element_type=jnp.float32,
            ),
            jnp.dot(
                owned,
                lax.all_gather(proj_dt, "seq", axis=0, tiled=True),
                preferred_element_type=jnp.float32,
            ),
        ),
        "fsdp",
    )
    bc_next = bc_sum.astype(jnp.bfloat16)
    bias_local = lax.dynamic_slice_in_dim(dt_bias, first_head, heads_dev, 0)
    decay_local = lax.dynamic_slice_in_dim(decay_rate, first_head, heads_dev, 0)
    skip_local = lax.dynamic_slice_in_dim(skip_gain, first_head, heads_dev, 0)
    dt_next = jax.nn.softplus(
        lax.dynamic_slice_in_dim(dt_sum, first_head, heads_dev, 1) + bias_local
    )
    offset = lax.axis_index("seq") * tokens_dev
    nblocks = tokens_dev // SPAN
    unit_decay = jnp.ones((heads_dev,), jnp.float32)
    zero_state = jnp.zeros((heads_dev, flat_size), jnp.float32)
    inputs = values_next.reshape(nblocks, SPAN, heads_dev, head_dim)
    marks_next = segment_marks(seg_next, offset, tokens_dev)
    b_vectors, c_vectors = pick_groups(bc_next, first_group, groups_dev, nblocks)
    mixing, send_factor, read_factor, carry_decay = block_parts(
        b_vectors, c_vectors, dt_next.reshape(nblocks, SPAN, heads_dev), marks_next, decay_local
    )
    scaled = (inputs.astype(jnp.float32) * send_factor[:, :, :, None]).astype(jnp.bfloat16)
    local_sums = outer_sum(scaled, b_vectors)
    summary = (unit_decay, zero_state)
    for block_id in range(nblocks):
        summary = joined(summary, (carry_decay[block_id], local_sums[block_id]))
    arrived = entering_2((summary[0], summary[1]), "seq", joined, (unit_decay, zero_state), False)
    state_now = arrived[1]
    starts_list = []
    for block_id in range(nblocks):
        starts_list.append(state_now)
        if block_id + 1 < nblocks:
            state_now = carry_decay[block_id][:, None] * state_now + local_sums[block_id]
    entering = jnp.stack(starts_list).reshape(nblocks, heads_dev, head_dim, state_dim)
    inside = jnp.einsum("khts,kshp->kthp", mixing, inputs, preferred_element_type=jnp.float32)
    output = (
        inside
        + read_state(entering, c_vectors, read_factor)
        + skip_local[:, None] * inputs.astype(jnp.float32)
    )
    out_next = output.astype(jnp.bfloat16).reshape(tokens_dev, heads_dev * head_dim)
    grads_in = grad_prev.reshape(nblocks, SPAN, heads_dev, head_dim)
    marks_prev = segment_marks(seg_prev, offset, tokens_dev)
    b_back, c_back = pick_groups(bc_prev, first_group, groups_dev, nblocks)
    mixing_back, send_back, read_back, carry_back = block_parts(
        b_back, c_back, dt_prev.reshape(nblocks, SPAN, heads_dev), marks_prev, decay_local
    )
    scaled_back = (grads_in.astype(jnp.float32) * read_back[:, :, :, None]).astype(jnp.bfloat16)
    local_back = outer_sum(scaled_back, c_back)
    summary_back = (unit_decay, zero_state)
    for block_id in reversed(range(nblocks)):
        summary_back = joined(summary_back, (carry_back[block_id], local_back[block_id]))
    arrived_back = entering_2(
        (summary_back[0], summary_back[1]), "seq", joined, (unit_decay, zero_state), True
    )
    state_back = arrived_back[1]
    ends_list = [zero_state] * nblocks
    for block_id in reversed(range(nblocks)):
        ends_list[block_id] = state_back
        if block_id > 0:
            state_back = carry_back[block_id][:, None] * state_back + local_back[block_id]
    leaving = jnp.stack(ends_list).reshape(nblocks, heads_dev, head_dim, state_dim)
    inside_back = jnp.einsum(
        "khts,kthp->kshp", mixing_back, grads_in, preferred_element_type=jnp.float32
    )
    gradient = (
        inside_back
        + read_state(leaving, b_back, send_back)
        + skip_local[:, None] * grads_in.astype(jnp.float32)
    )
    grad_values = gradient.astype(jnp.bfloat16).reshape(tokens_dev, heads_dev * head_dim)
    return (out_next, grad_values)


def solution(mesh):
    in_specs = (
        P("seq", None),
        P("seq", "fsdp"),
        P(),
        P(("seq", "fsdp"), None),
        P(("seq", "fsdp"), None),
        P(),
        P(),
        P(),
        P("seq", None),
        P("seq", "fsdp"),
        P(),
        P("seq", "fsdp"),
    )
    out_specs = (P("seq", "fsdp"), P("seq", "fsdp"))
    return jax.shard_map(body, mesh=mesh, in_specs=in_specs, out_specs=out_specs, check_vma=False)
```

profile of v0, /device:TPU:27, one launch (start us, length us, event | category | flops | bytes accessed | tf_op | source)
XLA Modules:
  0.0 551.0 jit_solution(4402773019058896170)
XLA Ops:
  7.9 6.4 %copy.160 = bf16[256,8192]{0,1:T(8,128)(2,1)} copy(bf16[256,8192]{1,0:T(8,128)(2,1)} %param.16) | data formatting | bytes 8388608 | tf_op args[0]
  14.3 1.7 constant_dynamic-slice_fusion.4
  16.1 31.3 %all-gather.7.cloned.1.call-done = bf16[4096,128]{1,0:T(8,128)(2,1)} async-done(((bf16[256,128]{1,0:T(8,128)(2,1)}), bf16[4096,128]{1,0:T(8,128)(2,1)}) %all-gather.7.cloned.1.call-update) | async-done | bytes 1048592 | tf_op jit(solution)/shard_map/all_gather | solution.py:135
  47.4 2.5 fusion.48
  51.3 4.3 copy.191
  55.6 5.8 %reshape.436 = f32[2,128,2,32,64]{1,0,4,3,2:T(2,128)} reshape(f32[256,4096]{0,1:T(8,128)} %copy.191) | data formatting | bytes 8388608 | tf_op jit(solution)/shard_map/convert_element_type | solution.py:184
  63.1 8.7 %all-reduce.3.cloned.1.call-done = f32[256,128]{0,1:T(8,128)} async-done(((f32[256,128]{0,1:T(8,128)}), f32[256,128]{0,1:T(8,128)}) %all-reduce.3.cloned.1.call-update) | async-done | bytes 131088 | tf_op jit(solution)/shard_map/psum | solution.py:126
  71.9 0.9 compare_select_fusion
  73.2 0.8 multiply_multiply_fusion
  74.1 4.5 multiply_convert_fusion.4
  79.3 1.8 fusion.46
  81.1 1.7 squeeze.53
  83.3 3.1 squeeze.54
  87.0 3.2 multiply_add_fusion
  90.6 1.2 copy-done.5
  91.8 2.9 copy.170
  94.8 5.8 %reshape.434 = f32[2,128,2,32,64]{1,0,4,3,2:T(2,128)} reshape(f32[256,4096]{0,1:T(8,128)} %copy.170) | data formatting | bytes 8388608 | tf_op jit(solution)/shard_map/convert_element_type | solution.py:158
  102.8 6.0 %multiply_convert_fusion.5 = bf16[2,128,2,32,64]{1,0,4,3,2:T(2,128)(2,1)} fusion(f32[2,128,2,32,64]{1,0,4,3,2:T(2,128)} %reshape.434, f32[2,128,2,32]{1,0,3,2:T(2,128)S(1)} %copy.173), kind=kLoop, calls=%fused_computation.26 | loop fusion | flops 2097152 | bytes 6356992 | tf_op jit(solution)/shard_map/convert_element_type | solution.py:158
  108.8 38.2 %all-gather.9.cloned.1.call-done = bf16[4096,1024]{1,0:T(8,128)(2,1)} async-done(((bf16[256,1024]{1,0:T(8,128)(2,1)}), bf16[4096,1024]{1,0:T(8,128)(2,1)}) %all-gather.9.cloned.1.call-update) | async-done | bytes 8388624 | tf_op jit(solution)/shard_map/all_gather | solution.py:130
  146.9 5.7 %fusion.49 = f32[256,1024]{1,0:T(8,128)S(1)} fusion(bf16[256,4096]{0,1:T(8,128)(2,1)S(1)} %bitcast.158, bf16[4096,1024]{1,0:T(8,128)(2,1)} %all-gather.9.cloned.1.call-done), kind=kOutput, calls=%fused_computation.109 | convolution fusion | flops 2147483648 | bytes 11534336 | tf_op jit(solution)/shard_map/dot_general | solution.py:128
  152.7 29.2 %all-reduce.4 = bf16[256,1024]{1,0:T(8,128)(2,1)} all-reduce(f32[256,1024]{1,0:T(8,128)S(1)} %fusion.49), channel_id=1, replica_groups=mesh['seq'=16,'fsdp'=2] {'fsdp'}, use_global_device_ids=true, to_apply=%region_4.5 | all-reduce | flops 262144 | bytes 1572864 | tf_op jit(solution)/shard_map/psum | solution.py:126
  181.9 1.4 reshape.420
  184.3 1.8 fusion.47
  186.1 1.7 squeeze.49
  188.1 2.9 squeeze.50
  191.0 3.3 multiply_add_fusion.1
  194.4 1.6 copy-done.4
  196.0 5.5 reshape.448
  201.5 7.0 %reshape.447 = bf16[2,128,64,64]{3,2,1,0:T(8,128)(2,1)} reshape(bf16[256,4096]{1,0:T(8,128)(2,1)} %param.17) | data formatting | bytes 4194304 | tf_op jit(solution)/shard_map/reshape | solution.py:152
  209.9 6.6 %copy.190 = bf16[2,128,64,64]{1,3,2,0:T(8,128)(2,1)} copy(bf16[2,128,64,64]{3,2,1,0:T(8,128)(2,1)} %reshape.448) | data formatting | bytes 4194304 | tf_op jit(solution)/shard_map/reshape | solution.py:178
  216.5 6.6 %copy.169 = bf16[2,128,64,64]{1,3,2,0:T(8,128)(2,1)} copy(bf16[2,128,64,64]{3,2,1,0:T(8,128)(2,1)} %reshape.447) | data formatting | bytes 4194304 | tf_op jit(solution)/shard_map/reshape | solution.py:152
  223.2 0.8 compare_and_fusion
  225.2 19.6 %all-gather.1 = f32[16,1,64]{2,1,0:T(1,128)S(1)} all-gather(f32[1,1,64]{2,1,0:T(1,128)S(1)} %copy-done.24), channel_id=1, replica_groups=mesh['seq'=16,'fsdp'=2] {'seq'}, dimensions={0}, use_global_device_ids=true | all-gather | bytes 4352 | tf_op jit(solution)/shard_map/all_gather | solution.py:14
  244.9 19.2 %all-gather = f32[16,1,64]{2,1,0:T(1,128)S(1)} all-gather(f32[1,1,64]{2,1,0:T(1,128)S(1)} %copy-done.25), channel_id=1, replica_groups=mesh['seq'=16,'fsdp'=2] {'seq'}, dimensions={0}, use_global_device_ids=true | all-gather | bytes 4352 | tf_op jit(solution)/shard_map/all_gather | solution.py:14
  264.3 52.2 %all-gather.13.cloned.1.call-done = f32[16,64,8192]{2,1,0:T(8,128)} async-done(((f32[1,64,8192]{2,1,0:T(8,128)}), f32[16,64,8192]{2,1,0:T(8,128)}) %all-gather.13.cloned.1.call-update) | async-done | bytes 33554448 | tf_op jit(solution)/shard_map/all_gather | solution.py:14
  317.3 3.0 fusion.24
  321.1 2.1 fusion.6
  323.2 1.0 mul.348
  324.8 4.5 fusion.11
  329.3 6.5 %copy.215 = bf16[2,128,64,64]{3,2,1,0:T(8,128)(2,1)} copy(bf16[2,128,64,64]{1,3,2,0:T(8,128)(2,1)S(1)} %fusion.11) | data formatting | bytes 4194304
  335.8 6.7 %reshape.446 = bf16[256,4096]{1,0:T(8,128)(2,1)} reshape(bf16[2,128,64,64]{3,2,1,0:T(8,128)(2,1)} %copy.215) | data formatting | bytes 4194304
  342.6 143.5 %all-gather.11.cloned.1.call-done = f32[16,64,8192]{2,1,0:T(8,128)} async-done(((f32[1,64,8192]{2,1,0:T(8,128)}), f32[16,64,8192]{2,1,0:T(8,128)}) %all-gather.11.cloned.1.call-update) | async-done | bytes 33554448 | tf_op jit(solution)/shard_map/all_gather | solution.py:14
  486.2 32.8 %while.26 = (s32[]{:T(128)}, f32[64,8192]{1,0:T(8,128)S(1)}, s32[]{:T(128)}, f32[16,64]{1,0:T(8,128)S(1)}, f32[16,64,8192]{2,1,0:T(8,128)}, /*index=5*/s32[]{:T(128)}, s32[]{:T(128)}, s32[]{:T(128)}) while((s32[]{:T(128)}, f32[64,8192]{1,0:T(8,128)S(1)}, s32[]{:T(128)}, f32[16,64]{1,0:T(8,128)S(1)}, f32[16,64,8192]{2,1,0:T(8,128)}, ...), condition=%wide.region_6.7_spmd, body=%wide.region_5.6_spmd.sunk | while | flops 1048581 | bytes 6292351 | solution.py:23
  486.3 2.1 bitcast_add_fusion.8
  488.4 2.1 bitcast_add_fusion.8
  490.6 2.1 bitcast_add_fusion.8
  492.8 2.1 bitcast_add_fusion.8
  495.0 2.1 bitcast_add_fusion.8
  497.1 2.1 bitcast_add_fusion.8
  499.3 2.1 bitcast_add_fusion.8
  501.5 2.1 bitcast_add_fusion.8
  503.6 2.1 bitcast_add_fusion.8
  505.8 2.1 bitcast_add_fusion.8
  508.0 2.1 bitcast_add_fusion.8
  510.1 2.1 bitcast_add_fusion.8
  512.3 2.1 bitcast_add_fusion.8
  514.5 2.1 bitcast_add_fusion.8
  516.6 2.1 bitcast_add_fusion.8
  519.0 3.0 fusion.25
  522.8 2.1 fusion.2
  524.9 1.0 mul.319
  526.4 4.7 fusion.13
  531.2 6.4 %copy.210 = bf16[2,128,64,64]{3,2,1,0:T(8,128)(2,1)} copy(bf16[2,128,64,64]{1,3,2,0:T(8,128)(2,1)S(1)} %fusion.13) | data formatting | bytes 4194304
  537.6 6.6 %reshape.445 = bf16[256,4096]{1,0:T(8,128)(2,1)} reshape(bf16[2,128,64,64]{3,2,1,0:T(8,128)(2,1)} %copy.210) | data formatting | bytes 4194304
  (156 shorter events, 16.6 us)
Async XLA Ops:
  7.2 40.2 %all-gather.7.cloned.1.call-start = ((), (), s32[]{:S(2)}) async-start(), calls=%async_computation | async-start | bytes 1114112 | tf_op jit(solution)/shard_map/all_gather | solution.py:135
  7.9 64.0 %all-reduce.3.cloned.1.call-start = ((), (), s32[]{:S(2)}) async-start(), calls=%async_computation.1 | async-start | bytes 262144 | tf_op jit(solution)/shard_map/psum | solution.py:126
  16.0 34.9 %copy-start.2 = (bf16[256,16,1,256]{0,3,2,1:T(8,128)(2,1)}, bf16[256,16,1,256]{0,3,2,1:T(8,128)(2,1)S(1)}, u32[]{:S(2)}) copy-start(bf16[256,16,1,256]{0,3,2,1:T(8,128)(2,1)S(1)} %constant_dynamic-slice_fusion.4) | copy-start | bytes 6291460
  16.0 34.6 %copy-start.28 = (f32[128]{0:T(128)S(1)}, f32[128]{0:T(128)}, u32[]{:S(2)}) copy-start(f32[128]{0:T(128)} %param.21) | copy-start | bytes 1540
  16.1 34.7 %copy-start.29 = (f32[128]{0:T(128)S(1)}, f32[128]{0:T(128)}, u32[]{:S(2)}) copy-start(f32[128]{0:T(128)} %param.22) | copy-start | bytes 1540
  16.1 34.8 %copy-start.18 = (f32[256,64]{0,1:T(8,128)S(1)}, f32[256,64]{0,1:T(8,128)}, u32[]{:S(2)}) copy-start(f32[256,64]{0,1:T(8,128)} %param.25) | copy-start | bytes 196612
  47.4 3.6 copy-start.30
  47.4 3.7 copy-start.31
  49.9 97.0 %all-gather.9.cloned.1.call-start = ((), (), s32[]{:S(2)}) async-start(), calls=%async_computation.2 | async-start | bytes 8912896 | tf_op jit(solution)/shard_map/all_gather | solution.py:130
  50.6 265.9 %all-gather.13.cloned.1.call-start = ((), (), s32[]{:S(2)}) async-start(), calls=%async_computation.4 | async-start | bytes 35651584 | tf_op jit(solution)/shard_map/all_gather | solution.py:14
  55.6 5.8 %copy-start.15 = (bf16[256,1024]{1,0:T(8,128)(2,1)S(1)}, bf16[256,1024]{1,0:T(8,128)(2,1)}, u32[]{:S(2)}) copy-start(bf16[256,1024]{1,0:T(8,128)(2,1)} %param.24) | copy-start | bytes 1572868
  62.5 16.2 %copy-start.11 = (bf16[256,1,2,128]{3,0,2,1:T(8,128)(2,1)}, bf16[256,1,2,128]{3,0,2,1:T(8,128)(2,1)S(1)}, u32[]{:S(2)}) copy-start(bf16[256,1,2,128]{3,0,2,1:T(8,128)(2,1)S(1)} %copy.185) | copy-start | bytes 393220
  72.9 5.8 %copy-start.13 = (f32[2,128,64]{1,0,2:T(2,128)}, f32[2,128,64]{1,0,2:T(2,128)S(1)}, u32[]{:S(2)}) copy-start(f32[2,128,64]{1,0,2:T(2,128)S(1)} %reshape.419) | copy-start | bytes 196612
  81.1 2.1 copy-start
  83.3 3.7 copy-start.7
  90.2 1.6 copy-start.5
  90.2 395.8 %all-gather.11.cloned.1.call-start = ((), (), s32[]{:S(2)}) async-start(), calls=%async_computation.3 | async-start | bytes 35651584 | tf_op jit(solution)/shard_map/all_gather | solution.py:14
  102.8 44.1 %copy-start.3 = (bf16[256,16,1,256]{0,3,2,1:T(8,128)(2,1)S(1)}, bf16[256,16,1,256]{0,3,2,1:T(8,128)(2,1)}, u32[]{:S(2)}) copy-start(bf16[256,16,1,256]{0,3,2,1:T(8,128)(2,1)} %copy-done.2) | copy-start | bytes 6291460
  152.7 31.0 %copy-start.6 = (bf16[2,128,2,32,64]{1,0,4,3,2:T(2,128)(2,1)S(1)}, bf16[2,128,2,32,64]{1,0,4,3,2:T(2,128)(2,1)}, u32[]{:S(2)}) copy-start(bf16[2,128,2,32,64]{1,0,4,3,2:T(2,128)(2,1)} %multiply_convert_fusion.5) | copy-start | bytes 6291460
  186.1 2.0 copy-start.1
  188.1 2.9 copy-start.8
  188.1 2.9 copy-start.26
  188.1 2.9 copy-start.27
  194.4 1.6 copy-start.4
  201.5 7.0 %copy-start.16 = (bf16[256,1,2,128]{0,3,2,1:T(8,128)(2,1)S(1)}, bf16[256,1,2,128]{0,3,2,1:T(8,128)(2,1)}, u32[]{:S(2)}) copy-start(bf16[256,1,2,128]{0,3,2,1:T(8,128)(2,1)} %get-tuple-element.166) | copy-start | bytes 393220
  201.5 7.1 %copy-start.32 = (f32[128]{0:T(128)S(1)}, f32[128]{0:T(128)}, u32[]{:S(2)}) copy-start(f32[128]{0:T(128)} %param.23) | copy-start | bytes 1540
  216.5 7.4 %copy-start.12 = (bf16[256,1,2,128]{3,0,2,1:T(8,128)(2,1)S(1)}, bf16[256,1,2,128]{3,0,2,1:T(8,128)(2,1)}, u32[]{:S(2)}) copy-start(bf16[256,1,2,128]{3,0,2,1:T(8,128)(2,1)} %copy-done.11) | copy-start | bytes 393220
  216.5 7.6 %copy-start.17 = (f32[2,128,64]{2,1,0:T(8,128)S(1)}, f32[2,128,64]{2,1,0:T(8,128)}, u32[]{:S(2)}) copy-start(f32[2,128,64]{2,1,0:T(8,128)} %get-tuple-element.170) | copy-start | bytes 196612
  216.5 8.7 %copy-start.14 = (f32[2,128,64]{1,0,2:T(2,128)S(1)}, f32[2,128,64]{1,0,2:T(2,128)}, u32[]{:S(2)}) copy-start(f32[2,128,64]{1,0,2:T(2,128)} %copy-done.13) | copy-start | bytes 196612
  216.5 8.7 %copy-start.24 = (f32[1,1,64]{2,1,0:T(1,128)S(1)}, f32[1,1,64]{2,1,0:T(1,128)}, u32[]{:S(2)}) copy-start(f32[1,1,64]{2,1,0:T(1,128)} %get-tuple-element.186) | copy-start | bytes 772
  216.5 28.4 %copy-start.25 = (f32[1,1,64]{2,1,0:T(1,128)S(1)}, f32[1,1,64]{2,1,0:T(1,128)}, u32[]{:S(2)}) copy-start(f32[1,1,64]{2,1,0:T(1,128)} %get-tuple-element.189) | copy-start | bytes 772
  316.7 0.7 copy-start.23
  323.2 1.6 copy-start.10
  323.2 1.6 copy-start.19
  323.2 1.6 copy-start.20
  323.2 1.6 copy-start.22
  323.2 1.6 copy-start.33
  524.8 1.6 copy-start.9
  524.8 1.6 copy-start.21
Sparse Core Ops, SparseCore 0:
  10.1 37.2 all-gather.6
  50.2 21.6 all-reduce.2
  74.0 72.8 all-gather.8
  148.4 168.0 all-gather.12
  318.0 168.0 all-gather.10
where the time goes:
time: 558 us; the launch traced here: 551 us
  waiting for transfers between devices  275 us (49%)
  local copies, waits for them, and re-layouts  107 us (19%)
  blocking collectives  68.1 us (12%)
  other arithmetic  60.8 us (11%)
  matrix products  23.3 us (4%)
  between operations  14.6 us (3%)
    all_gather x2, waiting for transfers between devices, entering_2(): gathered = jax.tree.map(lambda a: lax.all_gather(a, axis), part)  196 us
    unnamed x81, local copies, waits for them, and re-layouts  39.6 us
    all_gather x2, blocking collectives, entering_2(): gathered = jax.tree.map(lambda a: lax.all_gather(a, axis), part)  38.8 us
    add x17, other arithmetic, joined(): return (earlier[0] * later[0], later[0][:, None] * earlier[1] + later[1])  38.4 us
    all_gather x1, waiting for transfers between devices, body(): lax.all_gather(proj_bc, 'seq', axis=0, tiled=True)  38.2 us
    all_gather x1, waiting for transfers between devices, body(): lax.all_gather(proj_dt, 'seq', axis=0, tiled=True)  31.3 us
    psum x1, blocking collectives, body(): lax.psum((jnp.dot(owned, lax.all_gather(proj_bc, 'seq', axis=0, tiled=Tru...  29.2 us
    reshape x2, local copies, waits for them, and re-layouts, body(): inputs = values_next.reshape(nblocks, SPAN, heads_dev, head_dim)  13.6 us
  transfers between devices with their start and end apart: 5, of which 5 were waited for; matrix products, arithmetic and copies ran while one was open for 23% of the time, Pallas kernels for 0%

commit v1 on v0

v1 whole, which is shorter than its diff:
```python
import functools

import jax
import jax.numpy as jnp
from jax import lax
from jax.experimental import pallas as pl
from jax.experimental.pallas import tpu as pltpu
from jax.sharding import PartitionSpec as P

GW = 4
SPAN = 128
LANES = 128
MESH = pl.DeviceIdType.MESH


def scan_kernel(
    back, count, nblocks, heads, groups, head_dim,
    len_ref, x_ref, p_ref, q_ref, dt_ref, decay_ref, skip_ref,
    out_ref,
    cum_s, cum_t, dt_t, fin_s, fout_s, fexp, inside, pre, keep, inbox, outbox, send_sem, recv_sem,
):
    me = lax.axis_index("seq")
    place = count - 1 - me if back else me
    nxt = me - 1 if back else me + 1
    prv = me + 1 if back else me - 1
    npair = heads * head_dim // LANES
    per = LANES // head_dim
    pair_group = npair // groups
    first, last = place == 0, place == count - 1

    barrier = pltpu.get_barrier_semaphore()

    @pl.when(jnp.logical_not(first))
    def _():
        pl.semaphore_signal(barrier, inc=1, device_id={"seq": prv}, device_id_type=MESH)

    @pl.when(jnp.logical_not(last))
    def _():
        pl.semaphore_signal(barrier, inc=1, device_id={"seq": nxt}, device_id_type=MESH)

    bound = []
    total = jnp.int32(0)
    for k in range(3):
        total = total + len_ref[k]
        bound.append(total)

    def seg_of(pos):
        s = jnp.zeros_like(pos)
        for b in bound:
            s = s + (b <= pos).astype(jnp.int32)
        return s

    slab = me * (nblocks * SPAN)
    dim0 = lax.broadcasted_iota(jnp.int32, (SPAN, SPAN), 0)
    dim1 = lax.broadcasted_iota(jnp.int32, (SPAN, SPAN), 1)
    lane = lax.broadcasted_iota(jnp.int32, (1, LANES), 1)
    tril = (dim0 >= dim1).astype(jnp.float32)

    def widen(a, c):
        res = a[:, c * per:c * per + 1]
        for k in range(1, per):
            res = jnp.where(lane >= k * head_dim, a[:, c * per + k:c * per + k + 1], res)
        return jnp.broadcast_to(res, (a.shape[0], LANES))

    for c in range(npair):
        pre[0, c] = jnp.zeros((LANES, LANES), jnp.float32)
        keep[0, c] = jnp.ones((1, LANES), jnp.float32)

    for step in range(nblocks):
        b = nblocks - 1 - step if back else step
        rows = slice(b * SPAN, (b + 1) * SPAN)
        dt = dt_ref[rows, :]
        cum = jnp.dot(tril, -(dt * decay_ref[...]), precision=lax.Precision.HIGHEST,
                      preferred_element_type=jnp.float32)
        end = cum[SPAN - 1:SPAN, :]
        cum_s[rows, :] = cum
        cum_t[b] = cum.T
        dt_t[b] = dt.T
        pos = slab + b * SPAN + lax.broadcasted_iota(jnp.int32, (SPAN, heads), 0)
        seg = seg_of(pos)
        edge = slab + b * SPAN + lax.broadcasted_iota(jnp.int32, (1, heads), 0) * 0
        seg_e = seg_of(edge + (SPAN - 1))
        seg_b = jnp.where(edge == 0, 0, seg_of(edge - 1))
        send = jnp.where(seg == seg_e, jnp.exp(end - cum), 0.0)
        read = jnp.where(seg == seg_b, jnp.exp(cum), 0.0)
        carry = jnp.where(seg_e == seg_b, jnp.exp(end), 0.0)
        f_in = read if back else send * dt
        fin_s[rows, :] = f_in
        fout_s[rows, :] = send * dt if back else read
        qt = [q_ref[rows, g * LANES:(g + 1) * LANES].T for g in range(groups)]
        for c in range(npair):
            cols = slice(c * LANES, (c + 1) * LANES)
            sent = (x_ref[rows, cols].astype(jnp.float32) * widen(f_in, c)).astype(jnp.bfloat16)
            loc = jnp.dot(qt[c // pair_group], sent, preferred_element_type=jnp.float32)
            wide = widen(carry, c)
            pre[step + 1, c] = wide * pre[step, c] + loc
            keep[step + 1, c] = wide * keep[step, c]

    def in_block():
        def one(b, _):
            start = pl.multiple_of(b * SPAN, SPAN)
            rows = pl.ds(start, SPAN)
            seg_i = seg_of(slab + start + dim0)
            seg_j = seg_of(slab + start + dim1)
            order = (dim1 >= dim0) if back else (dim1 <= dim0)
            bias = jnp.where((seg_i == seg_j) & order, 0.0, -jnp.inf)
            cum = cum_s[rows, :]
            dt = dt_ref[rows, :]
            f_out = fout_s[rows, :]
            for g in range(groups):
                gl = slice(g * LANES, (g + 1) * LANES)
                score = lax.dot_general(p_ref[rows, gl], q_ref[rows, gl], (((1,), (1,)), ((), ())),
                                        preferred_element_type=jnp.float32)
                for c in range(g * pair_group, (g + 1) * pair_group):
                    cols = slice(c * LANES, (c + 1) * LANES)
                    x = x_ref[rows, cols]
                    mixes, parts = [], []
                    for k in range(per):
                        h = c * per + k
                        col = cum[:, h:h + 1]
                        row = cum_t[b, h:h + 1, :]
                        spread = (row - col) if back else (col - row)
                        w = jnp.exp(spread + bias) * score
                        if not back:
                            w = w * dt_t[b, h:h + 1, :]
                        mixes.append(w.astype(jnp.bfloat16))
                        mine = (lane >= k * head_dim) & (lane < (k + 1) * head_dim)
                        parts.append(jnp.where(mine, x, jnp.zeros_like(x)))
                    acc = jnp.dot(jnp.concatenate(mixes, 1), jnp.concatenate(parts, 0),
                                  preferred_element_type=jnp.float32)
                    if back:
                        acc = acc * widen(dt, c)
                    inside[c, rows, :] = acc + widen(skip_ref[...], c) * x.astype(jnp.float32)
                    fexp[c, rows, :] = widen(f_out, c)
            return 0

        lax.fori_loop(0, nblocks, one, 0)

    def finish(c, state):
        g = c // pair_group
        cols = pl.ds(pl.multiple_of(c * LANES, LANES), LANES)
        gl = pl.ds(pl.multiple_of(g * LANES, LANES), LANES)
        for step in range(nblocks):
            b = nblocks - 1 - step if back else step
            rows = slice(b * SPAN, (b + 1) * SPAN)
            entering = (keep[step, c] * state + pre[step, c]).astype(jnp.bfloat16)
            y = jnp.dot(p_ref[rows, gl], entering, preferred_element_type=jnp.float32)
            out_ref[rows, cols] = (inside[c, rows, :] + fexp[c, rows, :] * y).astype(jnp.bfloat16)

    def hop(c):
        return pltpu.make_async_remote_copy(
            src_ref=outbox.at[c], dst_ref=inbox.at[c], send_sem=send_sem.at[c],
            recv_sem=recv_sem.at[c], device_id={"seq": nxt}, device_id_type=MESH)

    late = place >= 5

    @pl.when(first)
    def _():
        inbox[...] = jnp.zeros_like(inbox)

    pl.semaphore_wait(barrier, jnp.where(first, 0, 1) + jnp.where(last, 0, 1))

    def relay(c, _):
        @pl.when(jnp.logical_not(first))
        def _():
            hop(c).wait_recv()

        state = inbox[c].astype(jnp.float32)

        @pl.when(jnp.logical_not(last))
        def _():
            outbox[c] = (keep[nblocks, c] * state + pre[nblocks, c]).astype(jnp.bfloat16)
            hop(c).start()

        @pl.when(late)
        def _():
            finish(c, state)

        return 0

    def phase(ph, _):
        @pl.when(ph == jnp.where(late, 0, 1))
        def _():
            in_block()

        @pl.when(ph == 0)
        def _():
            lax.fori_loop(0, npair, relay, 0)

        return 0

    lax.fori_loop(0, 2, phase, 0)

    @pl.when(jnp.logical_not(late))
    def _():
        def one(c, _):
            finish(c, inbox[c].astype(jnp.float32))
            return 0

        lax.fori_loop(0, npair, one, 0)

    @pl.when(jnp.logical_not(last))
    def _():
        def one(c, _):
            hop(c).wait_send()
            return 0

        lax.fori_loop(0, npair, one, 0)


def scan_pass(back, lengths, x, p_vec, q_vec, dt, decay, skip):
    tokens, width = x.shape
    heads = dt.shape[1]
    groups = p_vec.shape[1] // LANES
    head_dim = width // heads
    nblocks = tokens // SPAN
    npair = width // LANES
    count = lax.axis_size("seq")
    vm = pl.BlockSpec(memory_space=pltpu.VMEM)
    f32, bf16 = jnp.float32, jnp.bfloat16
    return pl.pallas_call(
        functools.partial(scan_kernel, back, count, nblocks, heads, groups, head_dim),
        out_shape=jax.ShapeDtypeStruct((tokens, width), bf16),
        in_specs=[pl.BlockSpec(memory_space=pltpu.SMEM)] + [vm] * 6,
        out_specs=vm,
        scratch_shapes=[
            pltpu.VMEM((tokens, heads), f32),
            pltpu.VMEM((nblocks, heads, SPAN), f32),
            pltpu.VMEM((nblocks, heads, SPAN), f32),
            pltpu.VMEM((tokens, heads), f32),
            pltpu.VMEM((tokens, heads), f32),
            pltpu.VMEM((npair, tokens, LANES), f32),
            pltpu.VMEM((npair, tokens, LANES), f32),
            pltpu.VMEM((nblocks + 1, npair, LANES, LANES), f32),
            pltpu.VMEM((nblocks + 1, npair, 1, LANES), f32),
            pltpu.VMEM((npair, LANES, LANES), bf16),
            pltpu.VMEM((npair, LANES, LANES), bf16),
            pltpu.SemaphoreType.DMA((npair,)),
            pltpu.SemaphoreType.DMA((npair,)),
        ],
        compiler_params=pltpu.CompilerParams(
            collective_id=1 if back else 0, has_side_effects=True,
            vmem_limit_bytes=40 * 1024 * 1024),
        cost_estimate=pl.CostEstimate(
            flops=40_000_000_000, bytes_accessed=8 * tokens * width, transcendentals=0),
        name="back_pass" if back else "next_pass",
    )(lengths, x, p_vec, q_vec, dt, decay, skip)


def body(
    hidden_next, values_next, seg_next, proj_bc, proj_dt, dt_bias, decay_rate, skip_gain,
    bc_prev, dt_prev, seg_prev, grad_prev,
):
    tokens_dev = hidden_next.shape[0]
    bc_width = proj_bc.shape[1]
    heads_all = proj_dt.shape[1]
    fsdp_count = lax.axis_size("fsdp")
    fsdp_place = lax.axis_index("fsdp")
    seq_count = lax.axis_size("seq")
    heads_dev = heads_all // fsdp_count
    state_dim = bc_width // (2 * GW)
    per_group = heads_all // GW
    groups_dev = max(1, heads_dev // per_group)
    first_head = fsdp_place * heads_dev
    first_group = first_head // per_group
    rows_dev = proj_bc.shape[0]
    half = bc_width // 2
    gw = groups_dev * state_dim

    pieces = []
    for f in range(fsdp_count):
        g0 = (f * heads_dev // per_group) * state_dim
        pieces += [proj_bc[:, g0:g0 + gw], proj_bc[:, half + g0:half + g0 + gw],
                   proj_dt[:, f * heads_dev:(f + 1) * heads_dev]]
    cols = 2 * gw + heads_dev
    weights = lax.all_gather(jnp.concatenate(pieces, axis=1), "seq", axis=0, tiled=True)

    decay = lax.dynamic_slice_in_dim(decay_rate, first_head, heads_dev, 0)[None]
    skip = lax.dynamic_slice_in_dim(skip_gain, first_head, heads_dev, 0)[None]
    bias = lax.dynamic_slice_in_dim(dt_bias, first_head, heads_dev, 0)[None]

    b_prev = lax.dynamic_slice_in_dim(bc_prev, first_group * state_dim, gw, 1)
    c_prev = lax.dynamic_slice_in_dim(bc_prev, half + first_group * state_dim, gw, 1)
    grad_values = scan_pass(True, seg_prev, grad_prev, b_prev, c_prev, dt_prev, decay, skip)

    owned = lax.dynamic_slice_in_dim(
        hidden_next.reshape(tokens_dev, seq_count, fsdp_count, rows_dev), fsdp_place, 1, 2
    ).reshape(tokens_dev, seq_count * rows_dev)
    owned, grad_values = lax.optimization_barrier((owned, grad_values))
    if fsdp_count == 2:
        other = lax.dynamic_slice_in_dim(weights, (1 - fsdp_place) * cols, cols, 1)
        mine = lax.dynamic_slice_in_dim(weights, fsdp_place * cols, cols, 1)
        away = lax.ppermute(jnp.dot(owned, other, preferred_element_type=jnp.float32),
                            "fsdp", [(0, 1), (1, 0)])
        sums = jnp.dot(owned, mine, preferred_element_type=jnp.float32) + away
    else:
        sums = lax.psum_scatter(jnp.dot(owned, weights, preferred_element_type=jnp.float32),
                                "fsdp", scatter_dimension=1, tiled=True)
    b_next = sums[:, :gw].astype(jnp.bfloat16)
    c_next = sums[:, gw:2 * gw].astype(jnp.bfloat16)
    dt_next = jax.nn.softplus(sums[:, 2 * gw:] + bias)
    out_next = scan_pass(False, seg_next, values_next, c_next, b_next, dt_next, decay, skip)
    return (out_next, grad_values)


def solution(mesh):
    in_specs = (
        P("seq", None), P("seq", "fsdp"), P(), P(("seq", "fsdp"), None), P(("seq", "fsdp"), None),
        P(), P(), P(), P("seq", None), P("seq", "fsdp"), P(), P("seq", "fsdp"),
    )
    out_specs = (P("seq", "fsdp"), P("seq", "fsdp"))
    return jax.shard_map(body, mesh=mesh, in_specs=in_specs, out_specs=out_specs, check_vma=False)
```

time: 558 us -> 186 us (0.33)
  the two profiles are of different devices: /device:TPU:27 before, /device:TPU:31 now
where the time goes in v1:
time: 186 us
  Pallas kernels  70.3 us (38%)
  waiting for transfers between devices  69.1 us (37%)
  local copies, waits for them, and re-layouts  18.6 us (10%)
  between operations  14.2 us (8%)
  matrix products  13.4 us (7%)
    pallas_call x2, Pallas kernels, scan_pass(): pl.pallas_call(functools.partial(scan_kernel, back, count, nblocks, heads...  70.3 us
    all_gather x1, waiting for transfers between devices, body(): lax.all_gather(jnp.concatenate(pieces, axis=1), 'seq', axis=0, tiled=True)  60.2 us
    unnamed x22, local copies, waits for them, and re-layouts  10.6 us
    ppermute x1, waiting for transfers between devices, body(): lax.ppermute(jnp.dot(owned, other, preferred_element_type=jnp.float32), '...  8.96 us
    dot_general x1, matrix products, body(): jnp.dot(owned, other, preferred_element_type=jnp.float32)  7.75 us
    dot_general x1, matrix products, body(): sums = jnp.dot(owned, mine, preferred_element_type=jnp.float32) + away  5.65 us
  transfers between devices with their start and end apart: 2, of which 2 were waited for; matrix products, arithmetic and copies ran while one was open for 8% of the time, Pallas kernels for 10%

profile of v1, /device:TPU:31, one launch (start us, length us, event | category | flops | bytes accessed | tf_op | source)
XLA Modules:
  0.0 185.9 jit_solution(12621474584647156947)
XLA Ops:
  7.2 0.0 all-gather.2.cloned.1.call-start
  7.2 1.1 fusion.7
  8.4 1.0 fusion.9
  9.4 1.1 concatenate.3
  10.5 0.0 all-gather.2.cloned.1.call-update
  10.5 0.0 copy-start.5
  10.5 0.0 copy-start.6
  10.5 0.0 copy-start.7
  10.5 0.0 copy-start.4
  10.5 6.5 %copy.24 = bf16[256,8192]{0,1:T(8,128)(2,1)} copy(bf16[256,8192]{1,0:T(8,128)(2,1)} %param.12) | data formatting | bytes 8388608 | tf_op args[0]
  17.0 0.0 copy-done.5
  17.0 0.1 copy.25.dt_ref
  17.1 0.0 copy-done.6
  17.1 0.0 copy-done.7
  17.1 0.1 dynamic-slice_bitcast_fusion
  17.2 0.0 copy-done.4
  17.3 0.0 copy-start
  17.3 0.0 copy-start.2
  17.3 3.3 %constant_dynamic-slice_fusion.2 = bf16[256,16,1,256]{0,3,2,1:T(8,128)(2,1)} fusion(bf16[256,16,2,256]{0,3,2,1:T(8,128)(2,1)} %bitcast.8, s32[]{:T(128)S(6)} %select_n.29), kind=kLoop, calls=%fused_computation.10 | loop fusion | bytes 4194308 | tf_op jit(solution)/shard_map/dynamic_slice | solution.py:286
  20.5 0.0 copy-done
  20.5 0.0 copy-done.2
  20.5 19.3 %back_pass.1 = bf16[256,4096]{1,0:T(8,128)(2,1)S(1)} custom-call(s32[4]{0:T(128)S(1)} %copy-done.2, bf16[256,4096]{1,0:T(8,128)(2,1)S(1)} %copy-done, bf16[256,256]{1,0:T(8,128)(2,1)S(1)} %get-tuple-element.13.p_ref, bf16[256,256]{1,0:T(8,128)(2,1)S(1)} %get-tuple-element.12.q_ref, f32[256,64]{1,0:T(8,128)S(1)} %copy.25.dt_ref, ...), custom_call_target="tpu_custom_call" | custom-call | flops 40000000000 | bytes 8388608 | tf_op jit(solution)/shard_map/back_pass/pallas_call | solution.py:221
  39.8 0.0 copy-start.8
  39.9 60.2 %all-gather.2.cloned.1.call-done = bf16[4096,1152]{1,0:T(8,128)(2,1)} async-done(((bf16[256,1152]{1,0:T(8,128)(2,1)}), bf16[4096,1152]{1,0:T(8,128)(2,1)}) %all-gather.2.cloned.1.call-update) | async-done | bytes 9437200 | tf_op jit(solution)/shard_map/all_gather | solution.py:276
  100.0 7.7 %fusion = f32[256,576]{0,1:T(8,128)S(1)} fusion(bf16[256,4096]{0,1:T(8,128)(2,1)} %bitcast.9, bf16[4096,1152]{1,0:T(8,128)(2,1)} %all-gather.2.cloned.1.call-done, s32[]{:T(128)S(6)} %select_n.35), kind=kOutput, calls=%fused_computation | convolution fusion | flops 1207959552 | bytes 7929860 | tf_op jit(solution)/shard_map/dot_general | solution.py:293
  107.8 0.1 collective-permute-start
  107.9 0.0 copy-done.8
  107.9 0.1 dynamic_slice.31
  107.9 5.6 %fusion.2 = f32[256,576]{1,0:T(8,128)S(1)} fusion(bf16[256,4096]{0,1:T(8,128)(2,1)} %bitcast.10, bf16[4096,1152]{1,0:T(8,128)(2,1)} %all-gather.2.cloned.1.call-done, s32[]{:T(128)S(6)} %select_n.34), kind=kOutput, calls=%fused_computation.2 | convolution fusion | flops 1207959552 | bytes 7929860 | tf_op jit(solution)/shard_map/dot_general | solution.py:295
  113.6 0.0 copy-start.3
  113.6 9.0 %collective-permute-done = f32[256,576]{0,1:T(8,128)} collective-permute-done((f32[256,576]{0,1:T(8,128)S(1)}, f32[256,576]{0,1:T(8,128)}, u32[]{:S(2)}, u32[]{:S(2)}) %collective-permute-start) | collective-permute-done | bytes 589856 | tf_op jit(solution)/shard_map/ppermute | solution.py:293
  122.6 1.3 copy.27
  123.9 0.0 copy-start.1
  123.9 0.1 fusion.6
  124.0 0.1 compare_select_fusion.dt_ref
  124.1 0.0 copy-done.3
  124.1 1.4 copy-done.1
  125.5 51.0 %next_pass.1 = bf16[256,4096]{1,0:T(8,128)(2,1)S(1)} custom-call(s32[4]{0:T(128)S(1)} %copy-done.3, bf16[256,4096]{1,0:T(8,128)(2,1)S(1)} %copy-done.1, bf16[256,256]{1,0:T(8,128)(2,1)S(1)} %get-tuple-element.15.p_ref, bf16[256,256]{1,0:T(8,128)(2,1)S(1)} %get-tuple-element.14.q_ref, f32[256,64]{1,0:T(8,128)S(1)} %compare_select_fusion.dt_ref, ...), custom_call_target="tpu_custom_call" | custom-call | flops 40000000000 | bytes 8388608 | tf_op jit(solution)/shard_map/next_pass/pallas_call | solution.py:221
  176.5 1.3 copy.31
  177.8 1.3 copy.32
  (2 shorter events, 0.1 us)
Async XLA Ops:
  7.2 92.9 %all-gather.2.cloned.1.call-start = ((), (), s32[]{:S(2)}) async-start(), calls=%async_computation | async-start | bytes 10027008 | tf_op jit(solution)/shard_map/all_gather | solution.py:276
  10.5 6.5 %copy-start.5 = (f32[256,64]{0,1:T(8,128)S(1)}, f32[256,64]{0,1:T(8,128)}, u32[]{:S(2)}) copy-start(f32[256,64]{0,1:T(8,128)} %param.21) | copy-start | bytes 196612
  10.5 6.6 %copy-start.6 = (f32[128]{0:T(128)S(1)}, f32[128]{0:T(128)}, u32[]{:S(2)}) copy-start(f32[128]{0:T(128)} %param.19) | copy-start | bytes 1540
  10.5 6.6 %copy-start.7 = (f32[128]{0:T(128)S(1)}, f32[128]{0:T(128)}, u32[]{:S(2)}) copy-start(f32[128]{0:T(128)} %param.18) | copy-start | bytes 1540
  10.5 6.7 %copy-start.4 = (bf16[256,1024]{1,0:T(8,128)(2,1)S(1)}, bf16[256,1024]{1,0:T(8,128)(2,1)}, u32[]{:S(2)}) copy-start(bf16[256,1024]{1,0:T(8,128)(2,1)} %param.20) | copy-start | bytes 1572868
  17.3 3.3 %copy-start = (bf16[256,4096]{1,0:T(8,128)(2,1)S(1)}, bf16[256,4096]{1,0:T(8,128)(2,1)}, u32[]{:S(2)}) copy-start(bf16[256,4096]{1,0:T(8,128)(2,1)} %x_ref.2) | copy-start | bytes 6291460
  17.3 3.3 %copy-start.2 = (s32[4]{0:T(128)S(1)}, s32[4]{0:T(128)}, u32[]{:S(2)}) copy-start(s32[4]{0:T(128)} %len_ref.2) | copy-start | bytes 52
  39.8 68.0 %copy-start.8 = (f32[128]{0:T(128)S(1)}, f32[128]{0:T(128)}, u32[]{:S(2)}) copy-start(f32[128]{0:T(128)} %param.17) | copy-start | bytes 1540
  107.8 14.8 %collective-permute-start = (f32[256,576]{0,1:T(8,128)S(1)}, f32[256,576]{0,1:T(8,128)}, u32[]{:S(2)}, u32[]{:S(2)}) collective-permute-start(f32[256,576]{0,1:T(8,128)S(1)} %fusion), channel_id=1, source_target_pairs={{0,1},{1,0},{2,3},{3,2},{4,5},{5,4},{6,7},{7,6},{8,9},{9,8},{10,11... | collective-permute-start | bytes 1769480 | tf_op jit(solution)/shard_map/ppermute | solution.py:293
  113.6 10.5 %copy-start.3 = (s32[4]{0:T(128)S(1)}, s32[4]{0:T(128)}, u32[]{:S(2)}) copy-start(s32[4]{0:T(128)} %len_ref.3) | copy-start | bytes 52
  123.9 1.6 copy-start.1
Sparse Core Ops, SparseCore 0:
  10.8 89.1 all-gather.1

commit v2 on v1

v2 whole, which is shorter than its diff:
```python
import functools

import jax
import jax.numpy as jnp
from jax import lax
from jax.experimental import pallas as pl
from jax.experimental.pallas import tpu as pltpu
from jax.sharding import PartitionSpec as P

GW = 4
SPAN = 128
LANES = 128
MESH = pl.DeviceIdType.MESH


def widen(a, c, head_dim):
    per = LANES // head_dim
    lane = lax.broadcasted_iota(jnp.int32, (1, LANES), 1)
    res = a[:, c * per:c * per + 1]
    for k in range(1, per):
        res = jnp.where(lane >= k * head_dim, a[:, c * per + k:c * per + k + 1], res)
    return jnp.broadcast_to(res, (a.shape[0], LANES))


def seg_maker(len_ref):
    bound = []
    total = jnp.int32(0)
    for k in range(len_ref.shape[0] - 1):
        total = total + len_ref[k]
        bound.append(total)

    def seg_of(pos):
        s = jnp.zeros_like(pos)
        for b in bound:
            s = s + (b <= pos).astype(jnp.int32)
        return s

    return seg_of


def local_states(back, dims, len_ref, x_ref, q_ref, dt_ref, decay_ref, work, pre, keep):
    nblocks, heads, groups, head_dim = dims
    cum_s, cum_t, dt_t, fout_s = work
    npair = heads * head_dim // LANES
    pair_group = npair // groups
    seg_of = seg_maker(len_ref)
    slab = lax.axis_index("seq") * (nblocks * SPAN)
    dim0 = lax.broadcasted_iota(jnp.int32, (SPAN, SPAN), 0)
    dim1 = lax.broadcasted_iota(jnp.int32, (SPAN, SPAN), 1)
    tril = (dim0 >= dim1).astype(jnp.float32)
    for c in range(npair):
        pre[0, c] = jnp.zeros((LANES, LANES), jnp.float32)
        keep[0, c] = jnp.ones((1, LANES), jnp.float32)
    for step in range(nblocks):
        b = nblocks - 1 - step if back else step
        rows = slice(b * SPAN, (b + 1) * SPAN)
        dt = dt_ref[rows, :]
        cum = jnp.dot(tril, -(dt * decay_ref[...]), precision=lax.Precision.HIGHEST,
                      preferred_element_type=jnp.float32)
        end = cum[SPAN - 1:SPAN, :]
        cum_s[rows, :] = cum
        cum_t[b] = cum.T
        dt_t[b] = dt.T
        seg = seg_of(slab + b * SPAN + lax.broadcasted_iota(jnp.int32, (SPAN, heads), 0))
        edge = slab + b * SPAN + lax.broadcasted_iota(jnp.int32, (1, heads), 0) * 0
        seg_e = seg_of(edge + (SPAN - 1))
        seg_b = jnp.where(edge == 0, 0, seg_of(edge - 1))
        send = jnp.where(seg == seg_e, jnp.exp(end - cum), 0.0) * dt
        read = jnp.where(seg == seg_b, jnp.exp(cum), 0.0)
        carry = jnp.where(seg_e == seg_b, jnp.exp(end), 0.0)
        f_in = read if back else send
        fout_s[rows, :] = send if back else read
        qt = [q_ref[rows, g * LANES:(g + 1) * LANES].T for g in range(groups)]
        for c in range(npair):
            cols = slice(c * LANES, (c + 1) * LANES)
            sent = (x_ref[rows, cols].astype(jnp.float32) * widen(f_in, c, head_dim)).astype(jnp.bfloat16)
            loc = jnp.dot(qt[c // pair_group], sent, preferred_element_type=jnp.float32)
            wide = widen(carry, c, head_dim)
            pre[step + 1, c] = wide * pre[step, c] + loc
            keep[step + 1, c] = wide * keep[step, c]


def in_block(back, dims, len_ref, x_ref, p_ref, q_ref, dt_ref, skip_ref, work, inside, fexp):
    nblocks, heads, groups, head_dim = dims
    cum_s, cum_t, dt_t, fout_s = work
    npair = heads * head_dim // LANES
    per = LANES // head_dim
    pair_group = npair // groups
    seg_of = seg_maker(len_ref)
    slab = lax.axis_index("seq") * (nblocks * SPAN)
    dim0 = lax.broadcasted_iota(jnp.int32, (SPAN, SPAN), 0)
    dim1 = lax.broadcasted_iota(jnp.int32, (SPAN, SPAN), 1)
    lane = lax.broadcasted_iota(jnp.int32, (1, LANES), 1)

    def one(b, _):
        start = pl.multiple_of(b * SPAN, SPAN)
        rows = pl.ds(start, SPAN)
        seg_i = seg_of(slab + start + dim0)
        seg_j = seg_of(slab + start + dim1)
        order = (dim1 >= dim0) if back else (dim1 <= dim0)
        bias = jnp.where((seg_i == seg_j) & order, 0.0, -jnp.inf)
        cum = cum_s[rows, :]
        dt = dt_ref[rows, :]
        f_out = fout_s[rows, :]
        for g in range(groups):
            gl = slice(g * LANES, (g + 1) * LANES)
            score = lax.dot_general(p_ref[rows, gl], q_ref[rows, gl], (((1,), (1,)), ((), ())),
                                    preferred_element_type=jnp.float32)
            for c in range(g * pair_group, (g + 1) * pair_group):
                cols = slice(c * LANES, (c + 1) * LANES)
                x = x_ref[rows, cols]
                mixes, parts = [], []
                for k in range(per):
                    h = c * per + k
                    col = cum[:, h:h + 1]
                    row = cum_t[b, h:h + 1, :]
                    spread = (row - col) if back else (col - row)
                    w = jnp.exp(spread + bias) * score
                    if not back:
                        w = w * dt_t[b, h:h + 1, :]
                    mixes.append(w.astype(jnp.bfloat16))
                    mine = (lane >= k * head_dim) & (lane < (k + 1) * head_dim)
                    parts.append(jnp.where(mine, x, jnp.zeros_like(x)))
                acc = jnp.dot(jnp.concatenate(mixes, 1), jnp.concatenate(parts, 0),
                              preferred_element_type=jnp.float32)
                if back:
                    acc = acc * widen(dt, c, head_dim)
                inside[c, rows, :] = acc + widen(skip_ref[...], c, head_dim) * x.astype(jnp.float32)
                fexp[c, rows, :] = widen(f_out, c, head_dim)
        return 0

    lax.fori_loop(0, nblocks, one, 0)


def back_kernel(dims, len_ref, x_ref, p_ref, q_ref, dt_ref, decay_ref, skip_ref,
                inside, fexp, pre, keep, *work):
    local_states(True, dims, len_ref, x_ref, q_ref, dt_ref, decay_ref, work, pre, keep)
    in_block(True, dims, len_ref, x_ref, p_ref, q_ref, dt_ref, skip_ref, work, inside, fexp)


HOP_CHUNKS = 5


def chain_kernel(count, dims, len_ref, x_ref, p_ref, q_ref, dt_ref, decay_ref, skip_ref,
                 pb_ref, inside_b, fexp_b, pre_b, keep_b,
                 out_ref, grad_ref, *scratch):
    work, rest = scratch[:4], scratch[4:]
    inside, fexp, pre, keep, inbox, outbox, in_b, out_b, s_sem, r_sem, sb_sem, rb_sem = rest
    nblocks, heads, groups, head_dim = dims
    npair = heads * head_dim // LANES
    pair_group = npair // groups
    me = lax.axis_index("seq")
    low, high = me == 0, me == count - 1

    barrier = pltpu.get_barrier_semaphore()

    @pl.when(jnp.logical_not(low))
    def _():
        pl.semaphore_signal(barrier, inc=1, device_id={"seq": me - 1}, device_id_type=MESH)

    @pl.when(jnp.logical_not(high))
    def _():
        pl.semaphore_signal(barrier, inc=1, device_id={"seq": me + 1}, device_id_type=MESH)

    local_states(False, dims, len_ref, x_ref, q_ref, dt_ref, decay_ref, work, pre, keep)

    @pl.when(low)
    def _():
        inbox[...] = jnp.zeros_like(inbox)

    @pl.when(high)
    def _():
        in_b[...] = jnp.zeros_like(in_b)

    pl.semaphore_wait(barrier, jnp.where(low, 0, 1) + jnp.where(high, 0, 1))

    def hop(back, c):
        return pltpu.make_async_remote_copy(
            src_ref=(out_b if back else outbox).at[c], dst_ref=(in_b if back else inbox).at[c],
            send_sem=(sb_sem if back else s_sem).at[c], recv_sem=(rb_sem if back else r_sem).at[c],
            device_id={"seq": me - 1 if back else me + 1}, device_id_type=MESH)

    def relay(back, c):
        first, last = (high, low) if back else (low, high)
        kp, pr = (keep_b, pre_b) if back else (keep, pre)

        @pl.when(jnp.logical_not(first))
        def _():
            hop(back, c).wait_recv()

        @pl.when(jnp.logical_not(last))
        def _():
            state = (in_b if back else inbox)[c].astype(jnp.float32)
            (out_b if back else outbox)[c] = (kp[nblocks, c] * state + pr[nblocks, c]).astype(jnp.bfloat16)
            hop(back, c).start()

    def finish(back, c):
        kp, pr, ins, fx, vec, out = (
            (keep_b, pre_b, inside_b, fexp_b, pb_ref, grad_ref) if back
            else (keep, pre, inside, fexp, p_ref, out_ref))
        g = c // pair_group
        cols = pl.ds(pl.multiple_of(c * LANES, LANES), LANES)
        gl = pl.ds(pl.multiple_of(g * LANES, LANES), LANES)
        state = (in_b if back else inbox)[c].astype(jnp.float32)
        for step in range(nblocks):
            b = nblocks - 1 - step if back else step
            rows = slice(b * SPAN, (b + 1) * SPAN)
            entering = (kp[step, c] * state + pr[step, c]).astype(jnp.bfloat16)
            y = jnp.dot(vec[rows, gl], entering, preferred_element_type=jnp.float32)
            out[rows, cols] = (ins[c, rows, :] + fx[c, rows, :] * y).astype(jnp.bfloat16)

    lag = (2 * me - (count - 1)) * HOP_CHUNKS
    up_first = lag < 0
    gap = jnp.where(up_first, -lag, lag)
    block_at = jnp.where(gap >= npair, npair, 0)

    def step_of(i, _):
        @pl.when(i == block_at)
        def _():
            in_block(False, dims, len_ref, x_ref, p_ref, q_ref, dt_ref, skip_ref, work, inside, fexp)

        for back in (False, True):
            leads = jnp.logical_not(up_first) if back else up_first
            c = i - jnp.where(leads, 0, gap)

            @pl.when((c >= 0) & (c < npair))
            def _(back=back, c=c):
                relay(back, c)

            done = jnp.where(leads, i - npair, c)

            @pl.when((done >= 0) & (done < npair))
            def _(back=back, done=done):
                finish(back, done)

        return 0

    lax.fori_loop(0, npair + jnp.maximum(gap, npair), step_of, 0)

    def drain(c, _):
        @pl.when(jnp.logical_not(high))
        def _():
            hop(False, c).wait_send()

        @pl.when(jnp.logical_not(low))
        def _():
            hop(True, c).wait_send()

        return 0

    lax.fori_loop(0, npair, drain, 0)


def sizes_of(x, p_vec, dt):
    tokens, width = x.shape
    heads = dt.shape[1]
    dims = (tokens // SPAN, heads, p_vec.shape[1] // LANES, width // heads)
    nblocks, npair = dims[0], width // LANES
    f32 = jnp.float32
    work = [pltpu.VMEM((tokens, heads), f32), pltpu.VMEM((nblocks, heads, SPAN), f32),
            pltpu.VMEM((nblocks, heads, SPAN), f32), pltpu.VMEM((tokens, heads), f32)]
    kept = [(npair, tokens, LANES), (npair, tokens, LANES),
            (nblocks + 1, npair, LANES, LANES), (nblocks + 1, npair, 1, LANES)]
    return dims, npair, work, kept


VM = pl.BlockSpec(memory_space=pltpu.VMEM)
SM = pl.BlockSpec(memory_space=pltpu.SMEM)


def back_parts(lengths, x, p_vec, q_vec, dt, decay, skip):
    dims, _, work, kept = sizes_of(x, p_vec, dt)
    return pl.pallas_call(
        functools.partial(back_kernel, dims),
        out_shape=[jax.ShapeDtypeStruct(k, jnp.float32) for k in kept],
        in_specs=[SM] + [VM] * 6,
        out_specs=[VM] * 4,
        scratch_shapes=work,
        compiler_params=pltpu.CompilerParams(vmem_limit_bytes=24 * 1024 * 1024),
        cost_estimate=pl.CostEstimate(flops=15_000_000_000, bytes_accessed=16_000_000, transcendentals=0),
        name="back_parts",
    )(lengths, x, p_vec, q_vec, dt, decay, skip)


def chains(lengths, x, p_vec, q_vec, dt, decay, skip, p_back, parts):
    dims, npair, work, kept = sizes_of(x, p_vec, dt)
    box = pltpu.VMEM((npair, LANES, LANES), jnp.bfloat16)
    sem = pltpu.SemaphoreType.DMA((npair,))
    return pl.pallas_call(
        functools.partial(chain_kernel, lax.axis_size("seq"), dims),
        out_shape=[jax.ShapeDtypeStruct(x.shape, jnp.bfloat16)] * 2,
        in_specs=[SM] + [VM] * 11,
        out_specs=[VM] * 2,
        scratch_shapes=work + [pltpu.VMEM(k, jnp.float32) for k in kept] + [box] * 4 + [sem] * 4,
        compiler_params=pltpu.CompilerParams(
            collective_id=0, has_side_effects=True, vmem_limit_bytes=56 * 1024 * 1024),
        cost_estimate=pl.CostEstimate(flops=40_000_000_000, bytes_accessed=40_000_000, transcendentals=0),
        name="chains",
    )(lengths, x, p_vec, q_vec, dt, decay, skip, p_back, *parts)


def body(
    hidden_next, values_next, seg_next, proj_bc, proj_dt, dt_bias, decay_rate, skip_gain,
    bc_prev, dt_prev, seg_prev, grad_prev,
):
    tokens_dev = hidden_next.shape[0]
    bc_width = proj_bc.shape[1]
    heads_all = proj_dt.shape[1]
    fsdp_count = lax.axis_size("fsdp")
    fsdp_place = lax.axis_index("fsdp")
    seq_count = lax.axis_size("seq")
    heads_dev = heads_all // fsdp_count
    state_dim = bc_width // (2 * GW)
    per_group = heads_all // GW
    groups_dev = max(1, heads_dev // per_group)
    first_head = fsdp_place * heads_dev
    first_group = first_head // per_group
    rows_dev = proj_bc.shape[0]
    half = bc_width // 2
    gw = groups_dev * state_dim

    pieces = []
    for f in range(fsdp_count):
        g0 = (f * heads_dev // per_group) * state_dim
        pieces += [proj_bc[:, g0:g0 + gw], proj_bc[:, half + g0:half + g0 + gw],
                   proj_dt[:, f * heads_dev:(f + 1) * heads_dev]]
    cols = 2 * gw + heads_dev
    weights = lax.all_gather(jnp.concatenate(pieces, axis=1), "seq", axis=0, tiled=True)

    decay = lax.dynamic_slice_in_dim(decay_rate, first_head, heads_dev, 0)[None]
    skip = lax.dynamic_slice_in_dim(skip_gain, first_head, heads_dev, 0)[None]
    bias = lax.dynamic_slice_in_dim(dt_bias, first_head, heads_dev, 0)[None]

    b_prev = lax.dynamic_slice_in_dim(bc_prev, first_group * state_dim, gw, 1)
    c_prev = lax.dynamic_slice_in_dim(bc_prev, half + first_group * state_dim, gw, 1)
    parts = back_parts(seg_prev, grad_prev, b_prev, c_prev, dt_prev, decay, skip)

    owned = lax.dynamic_slice_in_dim(
        hidden_next.reshape(tokens_dev, seq_count, fsdp_count, rows_dev), fsdp_place, 1, 2
    ).reshape(tokens_dev, seq_count * rows_dev)
    owned, parts = lax.optimization_barrier((owned, parts))
    if fsdp_count == 2:
        other = lax.dynamic_slice_in_dim(weights, (1 - fsdp_place) * cols, cols, 1)
        mine = lax.dynamic_slice_in_dim(weights, fsdp_place * cols, cols, 1)
        away = lax.ppermute(jnp.dot(owned, other, preferred_element_type=jnp.float32),
                            "fsdp", [(0, 1), (1, 0)])
        sums = jnp.dot(owned, mine, preferred_element_type=jnp.float32) + away
    else:
        sums = lax.psum_scatter(jnp.dot(owned, weights, preferred_element_type=jnp.float32),
                                "fsdp", scatter_dimension=1, tiled=True)
    b_next = sums[:, :gw].astype(jnp.bfloat16)
    c_next = sums[:, gw:2 * gw].astype(jnp.bfloat16)
    dt_next = jax.nn.softplus(sums[:, 2 * gw:] + bias)
    out_next, grad_values = chains(
        seg_next, values_next, c_next, b_next, dt_next, decay, skip, b_prev, parts)
    return (out_next, grad_values)


def solution(mesh):
    in_specs = (
        P("seq", None), P("seq", "fsdp"), P(), P(("seq", "fsdp"), None), P(("seq", "fsdp"), None),
        P(), P(), P(), P("seq", None), P("seq", "fsdp"), P(), P("seq", "fsdp"),
    )
    out_specs = (P("seq", "fsdp"), P("seq", "fsdp"))
    return jax.shard_map(body, mesh=mesh, in_specs=in_specs, out_specs=out_specs, check_vma=False)
```

time: 186 us -> 193 us (1.038)
  the two profiles are of different devices: /device:TPU:31 before, /device:TPU:0 now
where the time goes in v2:
time: 193 us; the launch traced here: 192 us
  Pallas kernels  72.9 us (38%)
  waiting for transfers between devices  62 us (32%)
  local copies, waits for them, and re-layouts  26.8 us (14%)
  between operations  14.2 us (7%)
  matrix products  13.7 us (7%)
    pallas_call x1, Pallas kernels, chains(): pl.pallas_call(functools.partial(chain_kernel, lax.axis_size('seq'), dims...  60.6 us
    all_gather x1, waiting for transfers between devices, body(): lax.all_gather(jnp.concatenate(pieces, axis=1), 'seq', axis=0, tiled=True)  53.6 us
    unnamed x34, local copies, waits for them, and re-layouts  19.2 us
    pallas_call x1, Pallas kernels, back_parts(): pl.pallas_call(functools.partial(back_kernel, dims), out_shape=[jax.Shape...  12.4 us
    ppermute x1, waiting for transfers between devices, body(): lax.ppermute(jnp.dot(owned, other, preferred_element_type=jnp.float32), '...  8.45 us
    dot_general x1, matrix products, body(): jnp.dot(owned, other, preferred_element_type=jnp.float32)  8.27 us
    dot_general x1, matrix products, body(): sums = jnp.dot(owned, mine, preferred_element_type=jnp.float32) + away  5.42 us
  transfers between devices with their start and end apart: 2, of which 2 were waited for; matrix products, arithmetic and copies ran while one was open for 8% of the time, Pallas kernels for 6%

profile of v2, /device:TPU:0, one launch (start us, length us, event | category | flops | bytes accessed | tf_op | source)
XLA Modules:
  0.0 192.3 jit_solution(1703193078985472185)
XLA Ops:
  7.2 0.0 all-gather.2.cloned.1.call-start
  7.2 1.0 fusion.9
  8.2 1.1 fusion.7
  9.4 1.1 concatenate.3
  10.5 0.0 all-gather.2.cloned.1.call-update
  10.5 0.9 copy.25.dt_ref
  11.5 0.0 copy-start.12
  11.5 0.0 copy-start.13
  11.5 0.0 copy-start.11
  11.5 6.4 %copy.24 = bf16[256,8192]{0,1:T(8,128)(2,1)} copy(bf16[256,8192]{1,0:T(8,128)(2,1)} %param.12) | data formatting | bytes 8388608 | tf_op args[0]
  17.9 0.0 copy-start.3
  17.9 0.0 copy-start.4
  17.9 0.0 copy-done.12
  17.9 0.0 copy-done.13
  17.9 0.1 dynamic-slice_bitcast_fusion
  18.0 0.0 copy-done.11
  18.0 0.0 copy-start.1
  18.0 0.0 copy-start.2
  18.1 0.0 copy-start
  18.1 3.2 %constant_dynamic-slice_fusion.2 = bf16[256,16,1,256]{0,3,2,1:T(8,128)(2,1)} fusion(bf16[256,16,2,256]{0,3,2,1:T(8,128)(2,1)} %bitcast.8, s32[]{:T(128)S(6)} %select_n.29), kind=kLoop, calls=%fused_computation.10 | loop fusion | bytes 4194308 | tf_op jit(solution)/shard_map/dynamic_slice | solution.py:338
  21.3 0.0 copy-done.3
  21.3 0.0 copy-done.4
  21.3 12.4 %back_parts.1 = (f32[32,256,128]{2,1,0:T(8,128)S(1)}, f32[32,256,128]{2,1,0:T(8,128)S(1)}, f32[3,32,128,128]{3,2,1,0:T(8,128)S(1)}, f32[3,32,1,128]{3,2,1,0:T(1,128)S(1)}) custom-call(s32[4]{0:T(128)S(1)} %copy-done.4, bf16[256,4096]{1,0:T(8,128)(2,1)S(1)} %copy-done.3, bf16[256,256]{1,0:T(8,128)(2,1)S(1)} %get-tuple-element.27.p_ref.pb_ref, ...), custom_call_target="tpu_custom_call" | custom-call | flops 15000000512 | bytes 16000000 | tf_op jit(solution)/shard_map/back_parts/pallas_call | solution.py:273
  33.7 0.0 copy-done.1
  33.7 0.0 copy-done.2
  33.7 0.0 copy-done
  33.7 0.0 copy-start.5
  33.7 2.6 %copy-done.5 = f32[3,32,128,128]{3,2,1,0:T(8,128)} copy-done((f32[3,32,128,128]{3,2,1,0:T(8,128)}, f32[3,32,128,128]{3,2,1,0:T(8,128)S(1)}, u32[]{:S(2)}) %copy-start.5) | copy-done | bytes 6291480
  36.4 0.0 copy-start.6
  36.4 1.9 %copy-done.6 = f32[32,256,128]{2,1,0:T(8,128)} copy-done((f32[32,256,128]{2,1,0:T(8,128)}, f32[32,256,128]{2,1,0:T(8,128)S(1)}, u32[]{:S(2)}) %copy-start.6) | copy-done | bytes 4194328
  38.3 0.0 copy-start.7
  38.3 2.0 %copy-done.7 = f32[32,256,128]{2,1,0:T(8,128)} copy-done((f32[32,256,128]{2,1,0:T(8,128)}, f32[32,256,128]{2,1,0:T(8,128)S(1)}, u32[]{:S(2)}) %copy-start.7) | copy-done | bytes 4194328
  40.3 0.0 copy-start.8
  40.3 0.6 copy-done.8
  40.9 0.0 copy-start.14
  40.9 0.0 copy-start.9
  40.9 53.6 %all-gather.2.cloned.1.call-done = bf16[4096,1152]{1,0:T(8,128)(2,1)} async-done(((bf16[256,1152]{1,0:T(8,128)(2,1)}), bf16[4096,1152]{1,0:T(8,128)(2,1)}) %all-gather.2.cloned.1.call-update) | async-done | bytes 9437200 | tf_op jit(solution)/shard_map/all_gather | solution.py:328
  94.5 8.3 %fusion = f32[256,576]{0,1:T(8,128)} fusion(bf16[256,4096]{0,1:T(8,128)(2,1)} %bitcast.9, bf16[4096,1152]{1,0:T(8,128)(2,1)} %all-gather.2.cloned.1.call-done, s32[]{:T(128)S(6)} %select_n.35), kind=kOutput, calls=%fused_computation | convolution fusion | flops 1207959552 | bytes 7929860 | tf_op jit(solution)/shard_map/dot_general | solution.py:345
  102.7 1.8 collective-permute-start
  104.5 0.0 copy-done.14
  104.5 0.1 dynamic_slice.31
  104.6 0.0 copy-done.9
  104.6 5.4 %fusion.2 = f32[256,576]{1,0:T(8,128)S(1)} fusion(bf16[256,4096]{0,1:T(8,128)(2,1)S(1)} %bitcast.10, bf16[4096,1152]{1,0:T(8,128)(2,1)} %all-gather.2.cloned.1.call-done, s32[]{:T(128)S(6)} %select_n.34), kind=kOutput, calls=%fused_computation.2 | convolution fusion | flops 1207959552 | bytes 7929860 | tf_op jit(solution)/shard_map/dot_general | solution.py:347
  110.0 8.4 %collective-permute-done = f32[256,576]{0,1:T(8,128)S(1)} collective-permute-done((f32[256,576]{0,1:T(8,128)}, f32[256,576]{0,1:T(8,128)S(1)}, u32[]{:S(2)}, u32[]{:S(2)}) %collective-permute-start) | collective-permute-done | bytes 589856 | tf_op jit(solution)/shard_map/ppermute | solution.py:345
  118.5 0.2 copy.27
  118.7 0.1 fusion.6
  118.8 0.7 fusion.8
  119.5 0.7 compare_select_fusion.dt_ref
  120.3 60.6 %chains.1 = (bf16[256,4096]{1,0:T(8,128)(2,1)}, bf16[256,4096]{1,0:T(8,128)(2,1)}) custom-call(s32[4]{0:T(128)} %len_ref.3, bf16[256,4096]{1,0:T(8,128)(2,1)} %x_ref.3, bf16[256,256]{1,0:T(8,128)(2,1)} %get-tuple-element.29.p_ref, bf16[256,256]{1,0:T(8,128)(2,1)} %get-tuple-element.28.q_ref, f32[256,64]{1,0:T(8,128)} %compare_select_fusion.dt_ref, ...), custom_call_target="tpu_custom_call" | custom-call | flops 40000000000 | bytes 40000000 | tf_op jit(solution)/shard_map/chains/pallas_call | solution.py:289
  180.8 0.0 copy-start.10
  180.8 3.3 %copy.31 = bf16[256,4096]{1,0:T(8,128)(2,1)} copy(bf16[256,4096]{1,0:T(8,128)(2,1)} %get-tuple-element.36) | data formatting | bytes 4194304
  184.1 0.0 copy-done.10
  184.1 1.3 copy.32
  (1 shorter events, 0.0 us)
Async XLA Ops:
  7.2 87.3 %all-gather.2.cloned.1.call-start = ((), (), s32[]{:S(2)}) async-start(), calls=%async_computation | async-start | bytes 10027008 | tf_op jit(solution)/shard_map/all_gather | solution.py:328
  11.5 6.5 %copy-start.12 = (f32[128]{0:T(128)S(1)}, f32[128]{0:T(128)}, u32[]{:S(2)}) copy-start(f32[128]{0:T(128)} %param.19) | copy-start | bytes 1540
  11.5 6.5 %copy-start.13 = (f32[128]{0:T(128)S(1)}, f32[128]{0:T(128)}, u32[]{:S(2)}) copy-start(f32[128]{0:T(128)} %param.18) | copy-start | bytes 1540
  11.5 6.5 %copy-start.11 = (bf16[256,1024]{1,0:T(8,128)(2,1)S(1)}, bf16[256,1024]{1,0:T(8,128)(2,1)}, u32[]{:S(2)}) copy-start(bf16[256,1024]{1,0:T(8,128)(2,1)} %param.20) | copy-start | bytes 1572868
  17.9 3.4 %copy-start.3 = (bf16[256,4096]{1,0:T(8,128)(2,1)S(1)}, bf16[256,4096]{1,0:T(8,128)(2,1)}, u32[]{:S(2)}) copy-start(bf16[256,4096]{1,0:T(8,128)(2,1)} %x_ref.2) | copy-start | bytes 6291460
  17.9 3.4 %copy-start.4 = (s32[4]{0:T(128)S(1)}, s32[4]{0:T(128)}, u32[]{:S(2)}) copy-start(s32[4]{0:T(128)} %len_ref.2) | copy-start | bytes 52
  18.0 15.7 %copy-start.1 = (f32[1,64]{1,0:T(1,128)}, f32[1,64]{1,0:T(1,128)S(1)}, u32[]{:S(2)}) copy-start(f32[1,64]{1,0:T(1,128)S(1)} %get-tuple-element.32.skip_ref) | copy-start | bytes 772
  18.0 15.7 %copy-start.2 = (f32[1,64]{1,0:T(1,128)}, f32[1,64]{1,0:T(1,128)S(1)}, u32[]{:S(2)}) copy-start(f32[1,64]{1,0:T(1,128)S(1)} %get-tuple-element.33.decay_ref) | copy-start | bytes 772
  18.1 15.6 %copy-start = (bf16[256,256]{1,0:T(8,128)(2,1)}, bf16[256,256]{1,0:T(8,128)(2,1)S(1)}, u32[]{:S(2)}) copy-start(bf16[256,256]{1,0:T(8,128)(2,1)S(1)} %get-tuple-element.27.p_ref.pb_ref) | copy-start | bytes 393220
  33.7 2.6 %copy-start.5 = (f32[3,32,128,128]{3,2,1,0:T(8,128)}, f32[3,32,128,128]{3,2,1,0:T(8,128)S(1)}, u32[]{:S(2)}) copy-start(f32[3,32,128,128]{3,2,1,0:T(8,128)S(1)} %get-tuple-element.18.pre_b) | copy-start | bytes 18874372
  36.4 1.9 %copy-start.6 = (f32[32,256,128]{2,1,0:T(8,128)}, f32[32,256,128]{2,1,0:T(8,128)S(1)}, u32[]{:S(2)}) copy-start(f32[32,256,128]{2,1,0:T(8,128)S(1)} %get-tuple-element.16.inside_b) | copy-start | bytes 12582916
  38.3 2.0 %copy-start.7 = (f32[32,256,128]{2,1,0:T(8,128)}, f32[32,256,128]{2,1,0:T(8,128)S(1)}, u32[]{:S(2)}) copy-start(f32[32,256,128]{2,1,0:T(8,128)S(1)} %get-tuple-element.17.fexp_b) | copy-start | bytes 12582916
  40.3 0.6 copy-start.8
  40.9 63.6 %copy-start.14 = (f32[128]{0:T(128)S(1)}, f32[128]{0:T(128)}, u32[]{:S(2)}) copy-start(f32[128]{0:T(128)} %param.17) | copy-start | bytes 1540
  40.9 63.7 %copy-start.9 = (bf16[256,16,1,256]{0,3,2,1:T(8,128)(2,1)S(1)}, bf16[256,16,1,256]{0,3,2,1:T(8,128)(2,1)}, u32[]{:S(2)}) copy-start(bf16[256,16,1,256]{0,3,2,1:T(8,128)(2,1)} %constant_dynamic-slice_fusion.2) | copy-start | bytes 6291460
  102.7 15.7 %collective-permute-start = (f32[256,576]{0,1:T(8,128)}, f32[256,576]{0,1:T(8,128)S(1)}, u32[]{:S(2)}, u32[]{:S(2)}) collective-permute-start(f32[256,576]{0,1:T(8,128)} %fusion), channel_id=1, source_target_pairs={{0,1},{1,0},{2,3},{3,2},{4,5},{5,4},{6,7},{7,6},{8,9},{9,8},{10,11... | collective-permute-start | bytes 1769480 | tf_op jit(solution)/shard_map/ppermute | solution.py:345
  180.8 3.3 %copy-start.10 = (bf16[256,4096]{1,0:T(8,128)(2,1)S(1)}, bf16[256,4096]{1,0:T(8,128)(2,1)}, u32[]{:S(2)}) copy-start(bf16[256,4096]{1,0:T(8,128)(2,1)} %get-tuple-element.37) | copy-start | bytes 6291460
Sparse Core Ops, SparseCore 0:
  10.8 83.6 all-gather.1

commit v3 on v2

--- a/solution.py
+++ b/solution.py
@@ -299,6 +299,149 @@
     )(lengths, x, p_vec, q_vec, dt, decay, skip, p_back, *parts)
 
 
+PIECES = 4
+
+
+def gather_kernel(count, h_ref, w_ref, bc_ref, dt_ref,
+                  held, acc, bc_out, bc_in, dt_out, dt_in,
+                  ring_s, ring_r, side_s, side_r, x_s, x_r):
+    me, f = lax.axis_index("seq"), lax.axis_index("fsdp")
+    n = count // 2
+    half_ring = n // 2
+    core, chip = me % 2, me // 2
+    r = jnp.where(chip % 2 == 0, chip // 2, n - 1 - chip // 2)
+    rows = w_ref.shape[0]
+    piece = rows // PIECES
+    wide = bc_ref.shape[1]
+
+    def id_of(pos, which):
+        p = (pos + 2 * n) % n
+        up = p < half_ring
+        return jnp.where(up, p * 2, (n - 1 - p) * 2 + 1) * 2 + which
+
+    nxt, prv, partner = id_of(r + 1, core), id_of(r - 1, core), chip * 2 + 1 - core
+
+    barrier = pltpu.get_barrier_semaphore()
+    for peer in (nxt, prv, partner):
+        pl.semaphore_signal(barrier, inc=1, device_id={"seq": peer}, device_id_type=MESH)
+    pl.semaphore_signal(barrier, inc=1, device_id={"fsdp": 1 - f}, device_id_type=MESH)
+    pl.semaphore_wait(barrier, 4)
+
+    def part(p):
+        return pl.ds(p * piece, piece)
+
+    def origin(step, p, which):
+        return id_of(r - step if p < PIECES // 2 else r + step, which)
+
+    def ring_copy(step, p, src):
+        return pltpu.make_async_remote_copy(
+            src_ref=src, dst_ref=held.at[origin(step, p, core), part(p), :],
+            send_sem=ring_s.at[step, p], recv_sem=ring_r.at[step, p],
+            device_id={"seq": nxt if p < PIECES // 2 else prv}, device_id_type=MESH)
+
+    def side_copy(step, p, src):
+        return pltpu.make_async_remote_copy(
+            src_ref=src, dst_ref=held.at[origin(step, p, core), part(p), :],
+            send_sem=side_s.at[step, p], recv_sem=side_r.at[step, p],
+            device_id={"seq": partner}, device_id_type=MESH)
+
+    def landed(step, p):
+        return held.at[origin(step, p, core), part(p), :]
+
+    for p in range(PIECES):
+        ring_copy(0, p, w_ref.at[part(p), :]).start()
+    for p in range(PIECES):
+        side_copy(0, p, w_ref.at[part(p), :]).start()
+
+    def columns(seq_index, first):
+        start = (seq_index * 2 + f) * rows + first
+        return h_ref[:, pl.ds(pl.multiple_of(start, rows // 2), rows // 2)]
+
+    def mac(step, which):
+        half = rows // 2
+        lo, hi = origin(step, 0, which), origin(step, PIECES - 1, which)
+        left = jnp.concatenate([columns(lo, 0), columns(hi, half)], axis=1)
+        right = jnp.concatenate([held[lo, 0:half, :], held[hi, half:, :]], axis=0)
+        acc[...] += jnp.dot(left, right, preferred_element_type=jnp.float32)
+
+    acc[...] = jnp.dot(jnp.concatenate([columns(me, 0), columns(me, rows // 2)], axis=1), w_ref[...],
+                       preferred_element_type=jnp.float32)
+
+    def one(step, _):
+        for p in (0, PIECES // 2, 1, PIECES // 2 + 1):
+            ring_copy(step, p, landed(step, p)).wait_recv()
+
+            @pl.when(step < n - 2)
+            def _(p=p):
+                ring_copy(step + 1, p, landed(step + 1, p)).start()
+
+            side_copy(step + 1, p, landed(step + 1, p)).start()
+        mac(step + 1, core)
+        for p in range(PIECES):
+            side_copy(step, p, landed(step, p)).wait_recv()
+        mac(step, 1 - core)
+        return 0
+
+    lax.fori_loop(0, n - 1, one, 0)
+    for p in range(PIECES):
+        side_copy(n - 1, p, landed(n - 1, p)).wait_recv()
+    mac(n - 1, 1 - core)
+
+    def cross(src, dst, k):
+        return pltpu.make_async_remote_copy(
+            src_ref=src, dst_ref=dst, send_sem=x_s.at[k], recv_sem=x_r.at[k],
+            device_id={"fsdp": 1 - f}, device_id_type=MESH)
+
+    def side_of(which):
+        return pl.ds(pl.multiple_of(which * wide, wide), wide)
+
+    bc_out[...] = acc[:, side_of(1 - f)].astype(jnp.bfloat16)
+    dt_out[...] = acc[:, 2 * wide:]
+    cross(bc_out, bc_in, 0).start()
+    cross(dt_out, dt_in, 1).start()
+
+    def drain(step, _):
+        for p in range(PIECES):
+            @pl.when(step < n - 1)
+            def _(p=p):
+                ring_copy(step, p, landed(step, p)).wait_send()
+
+            side_copy(step, p, landed(step, p)).wait_send()
+        return 0
+
+    lax.fori_loop(0, n, drain, 0)
+    cross(bc_out, bc_in, 0).wait()
+    bc_ref[...] = (acc[:, side_of(f)] + bc_in[...].astype(jnp.float32)).astype(jnp.bfloat16)
+    cross(dt_out, dt_in, 1).wait()
+    dt_ref[...] = acc[:, 2 * wide:] + dt_in[...]
+
+
+def gathered_sums(hidden, shard, wide):
+    count = lax.axis_size("seq")
+    tokens, total = hidden.shape[0], shard.shape[1]
+    f32, bf16 = jnp.float32, jnp.bfloat16
+    n = count // 2
+    dma = pltpu.SemaphoreType.DMA
+    return pl.pallas_call(
+        functools.partial(gather_kernel, count),
+        out_shape=[jax.ShapeDtypeStruct((tokens, wide), bf16),
+                   jax.ShapeDtypeStruct((tokens, total - 2 * wide), f32)],
+        in_specs=[VM] * 2,
+        out_specs=[VM] * 2,
+        scratch_shapes=[
+            pltpu.VMEM((count,) + shard.shape, bf16),
+            pltpu.VMEM((tokens, total), f32),
+            pltpu.VMEM((tokens, wide), bf16), pltpu.VMEM((tokens, wide), bf16),
+            pltpu.VMEM((tokens, total - 2 * wide), f32), pltpu.VMEM((tokens, total - 2 * wide), f32),
+            dma((n, PIECES)), dma((n, PIECES)), dma((n, PIECES)), dma((n, PIECES)), dma((2,)), dma((2,)),
+        ],
+        compiler_params=pltpu.CompilerParams(
+            collective_id=1, has_side_effects=True, vmem_limit_bytes=32 * 1024 * 1024),
+        cost_estimate=pl.CostEstimate(flops=40_000_000_000, bytes_accessed=40_000_000, transcendentals=0),
+        name="gather_project",
+    )(hidden, shard)
+
+
 def body(
     hidden_next, values_next, seg_next, proj_bc, proj_dt, dt_bias, decay_rate, skip_gain,
     bc_prev, dt_prev, seg_prev, grad_prev,
@@ -319,38 +462,37 @@
     half = bc_width // 2
     gw = groups_dev * state_dim
 
-    pieces = []
+    blocks = []
     for f in range(fsdp_count):
         g0 = (f * heads_dev // per_group) * state_dim
-        pieces += [proj_bc[:, g0:g0 + gw], proj_bc[:, half + g0:half + g0 + gw],
-                   proj_dt[:, f * heads_dev:(f + 1) * heads_dev]]
-    cols = 2 * gw + heads_dev
-    weights = lax.all_gather(jnp.concatenate(pieces, axis=1), "seq", axis=0, tiled=True)
+        blocks.append([proj_bc[:, g0:g0 + gw], proj_bc[:, half + g0:half + g0 + gw]])
+    ring = fsdp_count == 2 and seq_count % 4 == 0 and rows_dev % (2 * LANES) == 0 and heads_all == LANES
+    if ring:
+        shard = jnp.concatenate([*blocks[0], *blocks[1], proj_dt], axis=1)
+        bc_next, dt_sum = gathered_sums(hidden_next, shard, 2 * gw)
+        dt_sum = lax.dynamic_slice_in_dim(dt_sum, first_head, heads_dev, 1)
+    else:
+        pieces = []
+        for f in range(fsdp_count):
+            pieces += [*blocks[f], proj_dt[:, f * heads_dev:(f + 1) * heads_dev]]
+        weights = lax.all_gather(jnp.concatenate(pieces, axis=1), "seq", axis=0, tiled=True)
+        owned = lax.dynamic_slice_in_dim(
+            hidden_next.reshape(tokens_dev, seq_count, fsdp_count, rows_dev), fsdp_place, 1, 2
+        ).reshape(tokens_dev, seq_count * rows_dev)
+        sums = lax.psum_scatter(jnp.dot(owned, weights, preferred_element_type=jnp.float32),
+                                "fsdp", scatter_dimension=1, tiled=True)
+        bc_next, dt_sum = sums[:, :2 * gw].astype(jnp.bfloat16), sums[:, 2 * gw:]
 
     decay = lax.dynamic_slice_in_dim(decay_rate, first_head, heads_dev, 0)[None]
     skip = lax.dynamic_slice_in_dim(skip_gain, first_head, heads_dev, 0)[None]
     bias = lax.dynamic_slice_in_dim(dt_bias, first_head, heads_dev, 0)[None]
 
+    bc_prev, bc_next = lax.optimization_barrier((bc_prev, bc_next))
     b_prev = lax.dynamic_slice_in_dim(bc_prev, first_group * state_dim, gw, 1)
     c_prev = lax.dynamic_slice_in_dim(bc_prev, half + first_group * state_dim, gw, 1)
     parts = back_parts(seg_prev, grad_prev, b_prev, c_prev, dt_prev, decay, skip)
-
-    owned = lax.dynamic_slice_in_dim(
-        hidden_next.reshape(tokens_dev, seq_count, fsdp_count, rows_dev), fsdp_place, 1, 2
-    ).reshape(tokens_dev, seq_count * rows_dev)
-    owned, parts = lax.optimization_barrier((owned, parts))
-    if fsdp_count == 2:
-        other = lax.dynamic_slice_in_dim(weights, (1 - fsdp_place) * cols, cols, 1)
-        mine = lax.dynamic_slice_in_dim(weights, fsdp_place * cols, cols, 1)
-        away = lax.ppermute(jnp.dot(owned, other, preferred_element_type=jnp.float32),
-                            "fsdp", [(0, 1), (1, 0)])
-        sums = jnp.dot(owned, mine, preferred_element_type=jnp.float32) + away
-    else:
-        sums = lax.psum_scatter(jnp.dot(owned, weights, preferred_element_type=jnp.float32),
-                                "fsdp", scatter_dimension=1, tiled=True)
-    b_next = sums[:, :gw].astype(jnp.bfloat16)
-    c_next = sums[:, gw:2 * gw].astype(jnp.bfloat16)
-    dt_next = jax.nn.softplus(sums[:, 2 * gw:] + bias)
+    b_next, c_next = bc_next[:, :gw], bc_next[:, gw:]
+    dt_next = jax.nn.softplus(dt_sum + bias)
     out_next, grad_values = chains(
         seg_next, values_next, c_next, b_next, dt_next, decay, skip, b_prev, parts)
     return (out_next, grad_values)

time: 193 us -> 161 us (0.83)
  Pallas kernels: 72.9 us -> 138 us
  waiting for transfers between devices: 62 us -> 0 us
  matrix products: 13.7 us -> 0 us
  between operations: 14.2 us -> 0.75 us
  local copies, waits for them, and re-layouts: 26.8 us -> 21.8 us
    pallas_call x0 -> x1, Pallas kernels: none -> 63.1 us  [gathered_sums(): pl.pallas_call(functools.partial(gather_kernel, count), out_shape=[jax.Sh...]
    all_gather x1 -> x0, waiting for transfers between devices: 53.6 us -> none  [body(): lax.all_gather(jnp.concatenate(pieces, axis=1), 'seq', axis=0, tiled=True)]
    dot_general x2 -> x0, matrix products: 13.7 us -> none  [the longest x1 8.27 us: body(): jnp.dot(owned, other, preferred_element_type=jnp.float32)]
    ppermute x1 -> x0, waiting for transfers between devices: 8.45 us -> none  [body(): lax.ppermute(jnp.dot(owned, other, preferred_element_type=jnp.float32), '...]
    dynamic_slice x1 -> x0, local copies, waits for them, and re-layouts: 3.24 us -> none  [body(): lax.dynamic_slice_in_dim(hidden_next.reshape(tokens_dev, seq_count, fsdp_...]
    slice x3 -> x0, local copies, waits for them, and re-layouts: 2.86 us -> none  [the longest x1 1.14 us: body(): proj_bc[:, half + g0:half + g0 + gw]]
    unnamed x34 -> x31, local copies, waits for them, and re-layouts: 19.2 us -> 18.8 us
  transfers between devices with their start and end apart: 2 -> 0, of which waited for: 2 -> 0; matrix products, arithmetic and copies ran while one was open for 8% -> 0% of each run, Pallas kernels for 6% -> 0%
where the time goes in v3:
time: 161 us
  Pallas kernels  138 us (86%)
  local copies, waits for them, and re-layouts  21.8 us (14%)
    pallas_call x1, Pallas kernels, gathered_sums(): pl.pallas_call(functools.partial(gather_kernel, count), out_shape=[jax.Sh...  63.1 us
    pallas_call x1, Pallas kernels, chains(): pl.pallas_call(functools.partial(chain_kernel, lax.axis_size('seq'), dims...  62.4 us
    unnamed x31, local copies, waits for them, and re-layouts  18.8 us
    pallas_call x1, Pallas kernels, back_parts(): pl.pallas_call(functools.partial(back_kernel, dims), out_shape=[jax.Shape...  12.2 us

profile of v3, /device:TPU:0, one launch (start us, length us, event | category | flops | bytes accessed | tf_op | source)
XLA Modules:
  0.0 161.0 jit_solution(2908810659299816955)
XLA Ops:
  0.7 0.7 dynamic_slice.19
  1.4 0.7 dynamic-slice_bitcast_fusion
  2.1 0.0 copy-start.1
  2.1 0.0 copy-start.2
  2.1 0.9 copy.14.dt_ref
  3.1 0.9 slice_dynamic-update-slice_fusion.3
  4.0 0.9 slice_dynamic-update-slice_fusion.2
  4.9 0.9 slice_dynamic-update-slice_fusion.1
  5.8 0.9 slice_dynamic-update-slice_fusion
  6.8 0.9 constant_dynamic-update-slice_fusion.w_ref
  7.6 0.0 copy-start.3
  7.6 2.2 %copy-done.3 = bf16[256,8192]{1,0:T(8,128)(2,1)S(1)} copy-done((bf16[256,8192]{1,0:T(8,128)(2,1)S(1)}, bf16[256,8192]{1,0:T(8,128)(2,1)}, u32[]{:S(2)}) %copy-start.3) | copy-done | bytes 4194328
  9.8 0.0 copy-start.11
  9.8 0.0 copy-start.4
  9.8 0.0 copy-start.5
  9.8 63.1 %gather_project.1 = (bf16[256,512]{1,0:T(8,128)(2,1)S(1)}, f32[256,128]{1,0:T(8,128)S(1)}) custom-call(bf16[256,8192]{1,0:T(8,128)(2,1)S(1)} %copy-done.3, bf16[256,1152]{1,0:T(8,128)(2,1)S(1)} %constant_dynamic-update-slice_fusion.w_ref), custom_call_target="tpu_custom_call" | custom-call | flops 40000000000 | bytes 40000000 | tf_op jit(solution)/shard_map/gather_project/pallas_call | solution.py:425
  72.9 0.8 compare_select_fusion.dt_ref
  73.7 0.0 copy-done.11
  73.7 0.7 constant_dynamic-slice_fusion
  74.5 0.0 copy-start
  74.5 0.0 copy-done.1
  74.5 0.0 copy-done.2
  74.5 0.0 copy-done.4
  74.5 0.0 copy-done.5
  74.5 12.2 %back_parts.1 = (f32[32,256,128]{2,1,0:T(8,128)S(1)}, f32[32,256,128]{2,1,0:T(8,128)S(1)}, f32[3,32,128,128]{3,2,1,0:T(8,128)S(1)}, f32[3,32,1,128]{3,2,1,0:T(1,128)S(1)}) custom-call(s32[4]{0:T(128)S(1)} %copy-done.5, bf16[256,4096]{1,0:T(8,128)(2,1)S(1)} %copy-done.4, bf16[256,256]{1,0:T(8,128)(2,1)S(1)} %get-tuple-element.19.p_ref.pb_ref, ...), custom_call_target="tpu_custom_call" | custom-call | flops 15000000512 | bytes 16000000 | tf_op jit(solution)/shard_map/back_parts/pallas_call | solution.py:273
  86.7 0.0 copy-done
  86.7 0.0 copy-start.6
  86.7 2.7 %copy-done.6 = f32[3,32,128,128]{3,2,1,0:T(8,128)} copy-done((f32[3,32,128,128]{3,2,1,0:T(8,128)}, f32[3,32,128,128]{3,2,1,0:T(8,128)S(1)}, u32[]{:S(2)}) %copy-start.6) | copy-done | bytes 6291480
  89.4 0.0 copy-start.7
  89.4 2.0 %copy-done.7 = f32[32,256,128]{2,1,0:T(8,128)} copy-done((f32[32,256,128]{2,1,0:T(8,128)}, f32[32,256,128]{2,1,0:T(8,128)S(1)}, u32[]{:S(2)}) %copy-start.7) | copy-done | bytes 4194328
  91.4 0.0 copy-start.8
  91.4 2.1 %copy-done.8 = f32[32,256,128]{2,1,0:T(8,128)} copy-done((f32[32,256,128]{2,1,0:T(8,128)}, f32[32,256,128]{2,1,0:T(8,128)S(1)}, u32[]{:S(2)}) %copy-start.8) | copy-done | bytes 4194328
  93.4 0.0 copy-start.9
  93.4 0.6 copy-done.9
  94.1 62.4 %chains.1 = (bf16[256,4096]{1,0:T(8,128)(2,1)}, bf16[256,4096]{1,0:T(8,128)(2,1)}) custom-call(s32[4]{0:T(128)} %len_ref.3, bf16[256,4096]{1,0:T(8,128)(2,1)} %x_ref.3, bf16[256,256]{1,0:T(8,128)(2,1)} %get-tuple-element.22.p_ref, bf16[256,256]{1,0:T(8,128)(2,1)} %get-tuple-element.23.q_ref, f32[256,64]{1,0:T(8,128)} %compare_select_fusion.dt_ref, ...), custom_call_target="tpu_custom_call" | custom-call | flops 40000000000 | bytes 40000000 | tf_op jit(solution)/shard_map/chains/pallas_call | solution.py:289
  156.4 0.0 copy-start.10
  156.4 3.3 %copy.21 = bf16[256,4096]{1,0:T(8,128)(2,1)} copy(bf16[256,4096]{1,0:T(8,128)(2,1)} %get-tuple-element.28) | data formatting | bytes 4194304
  159.7 0.0 copy-done.10
  159.7 1.3 copy.22
Async XLA Ops:
  2.1 72.3 %copy-start.1 = (f32[1,64]{1,0:T(1,128)}, f32[1,64]{1,0:T(1,128)S(1)}, u32[]{:S(2)}) copy-start(f32[1,64]{1,0:T(1,128)S(1)} %get-tuple-element.24.skip_ref) | copy-start | bytes 772
  2.1 72.3 %copy-start.2 = (f32[1,64]{1,0:T(1,128)}, f32[1,64]{1,0:T(1,128)S(1)}, u32[]{:S(2)}) copy-start(f32[1,64]{1,0:T(1,128)S(1)} %get-tuple-element.25.decay_ref) | copy-start | bytes 772
  7.6 2.2 %copy-start.3 = (bf16[256,8192]{1,0:T(8,128)(2,1)S(1)}, bf16[256,8192]{1,0:T(8,128)(2,1)}, u32[]{:S(2)}) copy-start(bf16[256,8192]{1,0:T(8,128)(2,1)} %h_ref.1) | copy-start | bytes 12582916
  9.8 63.9 %copy-start.11 = (bf16[256,1024]{1,0:T(8,128)(2,1)S(1)}, bf16[256,1024]{1,0:T(8,128)(2,1)}, u32[]{:S(2)}) copy-start(bf16[256,1024]{1,0:T(8,128)(2,1)} %param.20) | copy-start | bytes 1572868
  9.8 64.7 %copy-start.4 = (bf16[256,4096]{1,0:T(8,128)(2,1)S(1)}, bf16[256,4096]{1,0:T(8,128)(2,1)}, u32[]{:S(2)}) copy-start(bf16[256,4096]{1,0:T(8,128)(2,1)} %x_ref.2) | copy-start | bytes 6291460
  9.8 64.7 %copy-start.5 = (s32[4]{0:T(128)S(1)}, s32[4]{0:T(128)}, u32[]{:S(2)}) copy-start(s32[4]{0:T(128)} %len_ref.2) | copy-start | bytes 52
  74.5 12.2 %copy-start = (bf16[256,256]{1,0:T(8,128)(2,1)}, bf16[256,256]{1,0:T(8,128)(2,1)S(1)}, u32[]{:S(2)}) copy-start(bf16[256,256]{1,0:T(8,128)(2,1)S(1)} %get-tuple-element.19.p_ref.pb_ref) | copy-start | bytes 393220
  86.7 2.7 %copy-start.6 = (f32[3,32,128,128]{3,2,1,0:T(8,128)}, f32[3,32,128,128]{3,2,1,0:T(8,128)S(1)}, u32[]{:S(2)}) copy-start(f32[3,32,128,128]{3,2,1,0:T(8,128)S(1)} %get-tuple-element.16.pre_b) | copy-start | bytes 18874372
  89.4 2.0 %copy-start.7 = (f32[32,256,128]{2,1,0:T(8,128)}, f32[32,256,128]{2,1,0:T(8,128)S(1)}, u32[]{:S(2)}) copy-start(f32[32,256,128]{2,1,0:T(8,128)S(1)} %get-tuple-element.14.inside_b) | copy-start | bytes 12582916
  91.4 2.1 %copy-start.8 = (f32[32,256,128]{2,1,0:T(8,128)}, f32[32,256,128]{2,1,0:T(8,128)S(1)}, u32[]{:S(2)}) copy-start(f32[32,256,128]{2,1,0:T(8,128)S(1)} %get-tuple-element.15.fexp_b) | copy-start | bytes 12582916
  93.4 0.6 copy-start.9
  156.4 3.3 %copy-start.10 = (bf16[256,4096]{1,0:T(8,128)(2,1)S(1)}, bf16[256,4096]{1,0:T(8,128)(2,1)}, u32[]{:S(2)}) copy-start(bf16[256,4096]{1,0:T(8,128)(2,1)} %get-tuple-element.29) | copy-start | bytes 6291460

commit v4 on v3

--- a/solution.py
+++ b/solution.py
@@ -132,19 +132,14 @@
     lax.fori_loop(0, nblocks, one, 0)
 
 
-def back_kernel(dims, len_ref, x_ref, p_ref, q_ref, dt_ref, decay_ref, skip_ref,
-                inside, fexp, pre, keep, *work):
-    local_states(True, dims, len_ref, x_ref, q_ref, dt_ref, decay_ref, work, pre, keep)
-    in_block(True, dims, len_ref, x_ref, p_ref, q_ref, dt_ref, skip_ref, work, inside, fexp)
-
-
 HOP_CHUNKS = 5
 
 
 def chain_kernel(count, dims, len_ref, x_ref, p_ref, q_ref, dt_ref, decay_ref, skip_ref,
-                 pb_ref, inside_b, fexp_b, pre_b, keep_b,
+                 lenb_ref, xb_ref, pb_ref, qb_ref, dtb_ref,
                  out_ref, grad_ref, *scratch):
-    work, rest = scratch[:4], scratch[4:]
+    work, work_b, rest = scratch[:4], scratch[4:8], scratch[12:]
+    inside_b, fexp_b, pre_b, keep_b = scratch[8:12]
     inside, fexp, pre, keep, inbox, outbox, in_b, out_b, s_sem, r_sem, sb_sem, rb_sem = rest
     nblocks, heads, groups, head_dim = dims
     npair = heads * head_dim // LANES
@@ -163,6 +158,7 @@
         pl.semaphore_signal(barrier, inc=1, device_id={"seq": me + 1}, device_id_type=MESH)
 
     local_states(False, dims, len_ref, x_ref, q_ref, dt_ref, decay_ref, work, pre, keep)
+    local_states(True, dims, lenb_ref, xb_ref, qb_ref, dtb_ref, decay_ref, work_b, pre_b, keep_b)
 
     @pl.when(low)
     def _():
@@ -218,6 +214,7 @@
         @pl.when(i == block_at)
         def _():
             in_block(False, dims, len_ref, x_ref, p_ref, q_ref, dt_ref, skip_ref, work, inside, fexp)
+            in_block(True, dims, lenb_ref, xb_ref, pb_ref, qb_ref, dtb_ref, skip_ref, work_b, inside_b, fexp_b)
 
         for back in (False, True):
             leads = jnp.logical_not(up_first) if back else up_first
@@ -268,35 +265,22 @@
 SM = pl.BlockSpec(memory_space=pltpu.SMEM)
 
 
-def back_parts(lengths, x, p_vec, q_vec, dt, decay, skip):
-    dims, _, work, kept = sizes_of(x, p_vec, dt)
-    return pl.pallas_call(
-        functools.partial(back_kernel, dims),
-        out_shape=[jax.ShapeDtypeStruct(k, jnp.float32) for k in kept],
-        in_specs=[SM] + [VM] * 6,
-        out_specs=[VM] * 4,
-        scratch_shapes=work,
-        compiler_params=pltpu.CompilerParams(vmem_limit_bytes=24 * 1024 * 1024),
-        cost_estimate=pl.CostEstimate(flops=15_000_000_000, bytes_accessed=16_000_000, transcendentals=0),
-        name="back_parts",
-    )(lengths, x, p_vec, q_vec, dt, decay, skip)
-
-
-def chains(lengths, x, p_vec, q_vec, dt, decay, skip, p_back, parts):
+def chains(lengths, x, p_vec, q_vec, dt, decay, skip, *back):
     dims, npair, work, kept = sizes_of(x, p_vec, dt)
     box = pltpu.VMEM((npair, LANES, LANES), jnp.bfloat16)
     sem = pltpu.SemaphoreType.DMA((npair,))
     return pl.pallas_call(
         functools.partial(chain_kernel, lax.axis_size("seq"), dims),
         out_shape=[jax.ShapeDtypeStruct(x.shape, jnp.bfloat16)] * 2,
-        in_specs=[SM] + [VM] * 11,
+        in_specs=[SM] + [VM] * 6 + [SM] + [VM] * 4,
         out_specs=[VM] * 2,
-        scratch_shapes=work + [pltpu.VMEM(k, jnp.float32) for k in kept] + [box] * 4 + [sem] * 4,
+        scratch_shapes=(work * 2 + [pltpu.VMEM(k, jnp.float32) for k in kept] * 2
+                        + [box] * 4 + [sem] * 4),
         compiler_params=pltpu.CompilerParams(
             collective_id=0, has_side_effects=True, vmem_limit_bytes=56 * 1024 * 1024),
         cost_estimate=pl.CostEstimate(flops=40_000_000_000, bytes_accessed=40_000_000, transcendentals=0),
         name="chains",
-    )(lengths, x, p_vec, q_vec, dt, decay, skip, p_back, *parts)
+    )(lengths, x, p_vec, q_vec, dt, decay, skip, *back)
 
 
 PIECES = 4
@@ -395,7 +379,7 @@
     def side_of(which):
         return pl.ds(pl.multiple_of(which * wide, wide), wide)
 
-    bc_out[...] = acc[:, side_of(1 - f)].astype(jnp.bfloat16)
+    bc_out[...] = acc[:, side_of(1 - f)]
     dt_out[...] = acc[:, 2 * wide:]
     cross(bc_out, bc_in, 0).start()
     cross(dt_out, dt_in, 1).start()
@@ -411,7 +395,7 @@
 
     lax.fori_loop(0, n, drain, 0)
     cross(bc_out, bc_in, 0).wait()
-    bc_ref[...] = (acc[:, side_of(f)] + bc_in[...].astype(jnp.float32)).astype(jnp.bfloat16)
+    bc_ref[...] = (acc[:, side_of(f)] + bc_in[...]).astype(jnp.bfloat16)
     cross(dt_out, dt_in, 1).wait()
     dt_ref[...] = acc[:, 2 * wide:] + dt_in[...]
 
@@ -431,7 +415,7 @@
         scratch_shapes=[
             pltpu.VMEM((count,) + shard.shape, bf16),
             pltpu.VMEM((tokens, total), f32),
-            pltpu.VMEM((tokens, wide), bf16), pltpu.VMEM((tokens, wide), bf16),
+            pltpu.VMEM((tokens, wide), f32), pltpu.VMEM((tokens, wide), f32),
             pltpu.VMEM((tokens, total - 2 * wide), f32), pltpu.VMEM((tokens, total - 2 * wide), f32),
             dma((n, PIECES)), dma((n, PIECES)), dma((n, PIECES)), dma((n, PIECES)), dma((2,)), dma((2,)),
         ],
@@ -487,14 +471,13 @@
     skip = lax.dynamic_slice_in_dim(skip_gain, first_head, heads_dev, 0)[None]
     bias = lax.dynamic_slice_in_dim(dt_bias, first_head, heads_dev, 0)[None]
 
-    bc_prev, bc_next = lax.optimization_barrier((bc_prev, bc_next))
     b_prev = lax.dynamic_slice_in_dim(bc_prev, first_group * state_dim, gw, 1)
     c_prev = lax.dynamic_slice_in_dim(bc_prev, half + first_group * state_dim, gw, 1)
-    parts = back_parts(seg_prev, grad_prev, b_prev, c_prev, dt_prev, decay, skip)
     b_next, c_next = bc_next[:, :gw], bc_next[:, gw:]
     dt_next = jax.nn.softplus(dt_sum + bias)
     out_next, grad_values = chains(
-        seg_next, values_next, c_next, b_next, dt_next, decay, skip, b_prev, parts)
+        seg_next, values_next, c_next, b_next, dt_next, decay, skip,
+        seg_prev, grad_prev, b_prev, c_prev, dt_prev)
     return (out_next, grad_values)
 
 

time: 161 us -> 154 us (0.957)
  local copies, waits for them, and re-layouts: 21.8 us -> 15.8 us
  Pallas kernels: 138 us -> 136 us
    pallas_call x1 -> x0, Pallas kernels: 12.2 us -> none  [back_parts(): pl.pallas_call(functools.partial(back_kernel, dims), out_shape=[jax.Shape...]
    unnamed x31 -> x13, local copies, waits for them, and re-layouts: 18.8 us -> 12 us
    pallas_call x1, Pallas kernels: 63.1 us -> 68.7 us  [gathered_sums(): pl.pallas_call(functools.partial(gather_kernel, count), out_shape=[jax.Sh...]
    pallas_call x1, Pallas kernels: 62.4 us -> 67.6 us  [chains(): pl.pallas_call(functools.partial(chain_kernel, lax.axis_size('seq'), dims...]
where the time goes in v4:
time: 154 us
  Pallas kernels  136 us (88%)
  local copies, waits for them, and re-layouts  15.8 us (10%)
    pallas_call x1, Pallas kernels, gathered_sums(): pl.pallas_call(functools.partial(gather_kernel, count), out_shape=[jax.Sh...  68.7 us
    pallas_call x1, Pallas kernels, chains(): pl.pallas_call(functools.partial(chain_kernel, lax.axis_size('seq'), dims...  67.6 us
    unnamed x13, local copies, waits for them, and re-layouts  12 us

profile of v4, /device:TPU:0, one launch (start us, length us, event | category | flops | bytes accessed | tf_op | source)
XLA Modules:
  0.0 153.6 jit_solution(7069709090662371676)
XLA Ops:
  0.7 0.7 dynamic_slice.19
  1.4 1.3 dynamic-slice_bitcast_fusion
  2.7 1.6 %copy.14.dtb_ref = f32[256,64]{1,0:T(8,128)} copy(f32[256,64]{0,1:T(8,128)} %param.21) | data formatting | bytes 131072 | tf_op args[9]
  4.3 0.9 slice_dynamic-update-slice_fusion.3
  5.2 0.9 slice_dynamic-update-slice_fusion.2
  6.2 0.9 slice_dynamic-update-slice_fusion.1
  7.1 0.9 slice_dynamic-update-slice_fusion
  8.0 0.9 constant_dynamic-update-slice_fusion.w_ref
  8.9 0.0 copy-start
  8.9 2.2 %copy-done = bf16[256,8192]{1,0:T(8,128)(2,1)S(1)} copy-done((bf16[256,8192]{1,0:T(8,128)(2,1)S(1)}, bf16[256,8192]{1,0:T(8,128)(2,1)}, u32[]{:S(2)}) %copy-start) | copy-done | bytes 4194328
  11.0 0.0 copy-start.2
  11.0 68.7 %gather_project.1 = (bf16[256,512]{1,0:T(8,128)(2,1)S(1)}, f32[256,128]{1,0:T(8,128)S(1)}) custom-call(bf16[256,8192]{1,0:T(8,128)(2,1)S(1)} %copy-done, bf16[256,1152]{1,0:T(8,128)(2,1)S(1)} %constant_dynamic-update-slice_fusion.w_ref), custom_call_target="tpu_custom_call" | custom-call | flops 40000000000 | bytes 40000000 | tf_op jit(solution)/shard_map/gather_project/pallas_call | solution.py:409
  79.8 0.8 compare_select_fusion.dt_ref
  80.6 0.0 copy-done.2
  80.6 0.8 constant_dynamic-slice_fusion
  81.4 67.6 %chains.1 = (bf16[256,4096]{1,0:T(8,128)(2,1)}, bf16[256,4096]{1,0:T(8,128)(2,1)}) custom-call(s32[4]{0:T(128)} %len_ref.1, bf16[256,4096]{1,0:T(8,128)(2,1)} %x_ref.1, bf16[256,256]{1,0:T(8,128)(2,1)} %get-tuple-element.12.p_ref, bf16[256,256]{1,0:T(8,128)(2,1)} %get-tuple-element.13.q_ref, f32[256,64]{1,0:T(8,128)} %compare_select_fusion.dt_ref, ...), custom_call_target="tpu_custom_call" | custom-call | flops 40000000000 | bytes 40000000 | tf_op jit(solution)/shard_map/chains/pallas_call | solution.py:272
  149.0 0.0 copy-start.1
  149.0 3.3 %copy.21 = bf16[256,4096]{1,0:T(8,128)(2,1)} copy(bf16[256,4096]{1,0:T(8,128)(2,1)} %get-tuple-element.16) | data formatting | bytes 4194304
  152.3 0.0 copy-done.1
  152.3 1.3 copy.22
Async XLA Ops:
  8.9 2.2 %copy-start = (bf16[256,8192]{1,0:T(8,128)(2,1)S(1)}, bf16[256,8192]{1,0:T(8,128)(2,1)}, u32[]{:S(2)}) copy-start(bf16[256,8192]{1,0:T(8,128)(2,1)} %h_ref.1) | copy-start | bytes 12582916
  11.0 69.6 %copy-start.2 = (bf16[256,1024]{1,0:T(8,128)(2,1)S(1)}, bf16[256,1024]{1,0:T(8,128)(2,1)}, u32[]{:S(2)}) copy-start(bf16[256,1024]{1,0:T(8,128)(2,1)} %param.20) | copy-start | bytes 1572868
  149.0 3.3 %copy-start.1 = (bf16[256,4096]{1,0:T(8,128)(2,1)S(1)}, bf16[256,4096]{1,0:T(8,128)(2,1)}, u32[]{:S(2)}) copy-start(bf16[256,4096]{1,0:T(8,128)(2,1)} %get-tuple-element.17) | copy-start | bytes 6291460
